TPU v7x, 512 devices: a whole 4x4x16 slice. The times are simulated.
512 devices in a mesh: rep: 4 (over y), ep: 128 (over z, x, core).
Axes of the slice: x: 4, y: 4, z: 16, core: 2. Of those that a mesh axis runs over, the one named last changes fastest.
Arguments:
- gen_cache: bfloat16 [4096, 32, 2, 4, 128], P(('rep', 'ep')), may hold values from -6 to 6
- prompt_cache: bfloat16 [256, 2, 4, 128], replicated, may hold values from -5 to 5
- ancestors: int32 [4096], P(('rep', 'ep')), may hold values from 0 to 1023, as said below
- queries: bfloat16 [4096, 2, 64, 128], P(('rep', 'ep')), may hold values from -5 to 5
- new_kv: bfloat16 [4096, 2, 2, 4, 128], P(('rep', 'ep')), may hold values from -6 to 6
- tokens_in: bfloat16 [4096, 2, 2048], P(('rep', 'ep')), may hold values from -6 to 6
- norm_gain: float32 [2048], replicated, may hold values from 0.1 to 1.9
- routes: int32 [4, 1024, 2, 8], P(None, 'ep'), may hold values from 0 to 127, all different within a row; in each aligned block of 16 rows (0 to 15, 16 to 31, ..., all dimensions but the last counted through in order) at most 2 rows name the same one
- gate_weights: float32 [4, 1024, 2, 8], P(None, 'ep'), may hold values from 0.1 to 1
- w_gate_up: bfloat16 [128, 2048, 2, 768], P('ep', None, None, 'rep'), may hold values from -0.125 to 0.125
- w_down: bfloat16 [128, 768, 2048], P('ep', 'rep'), may hold values from -0.21875 to 0.21875
Outputs:
- cache_out: bfloat16 [4096, 32, 2, 4, 128], P(('rep', 'ep'))
- attn_out: bfloat16 [4096, 2, 64, 128], P(('rep', 'ep'))
- expert_out: bfloat16 [4096, 2, 2048], P(('rep', 'ep'))
Inputs may be any that keep to these rules, and one draw needn't show every extreme that they name: The parent of particle p is particle (p // 1024) * 1024 + ancestors[p]. `routes`: each row names 8 different experts. In the rows of one device (aligned blocks of 16 rows, taking the leading dimensions together in order) no expert is named more than 2 times.
All inputs are finite; a program needn't handle non-finite values.
Results may differ from a plain program's by a relative error of at most 0.013.
Values may be sent and summed in bfloat16 or wider, within the bound.
No kernel may reach another device: no remote copies, remote signals or barrier semaphores. Data moves between devices by JAX's collectives and lax.ppermute only.
A program may use at most 64 MiB of HBM per device.

v0:
```python
import math

import jax
import jax.numpy as jnp
from jax import lax
from jax.sharding import Mesh
from jax.sharding import PartitionSpec as P

EP = ("ep_0", "ep_1", "ep_2")
REP_EP = ("rep", "ep_0", "ep_1", "ep_2")


def joined_along(tiles, dim):
    lengths = list(tiles.shape[1:])
    lengths[dim] *= tiles.shape[0]
    return jnp.moveaxis(tiles, 0, dim).reshape(lengths)


def gather_in_order(value, axes, order):
    tiles = value
    for k in order:
        tiles = lax.all_gather(tiles, axes[k])
    done = order[::-1]
    back = [done.index(k) for k in range(len(axes))]
    tiles = tiles.transpose(*back, *range(len(axes), tiles.ndim))
    return tiles.reshape(-1, *value.shape)


def gather_axes(value, axes, order, dim):
    return joined_along(gather_in_order(value, axes, order), dim)


def attend(queries, gen_block, new_block, prompt_cache):
    count = queries.shape[0]
    heads = queries.shape[2]
    head_dim = queries.shape[3]
    kv_heads = new_block.shape[3]
    score_scale = 1.0 / math.sqrt(head_dim)
    grouped = queries.reshape(count, 2, kv_heads, heads // kv_heads, head_dim)
    prompt_scores = (
        jnp.einsum(
            "btngd,snd->btngs", grouped, prompt_cache[:, 0], preferred_element_type=jnp.float32
        )
        * score_scale
    )
    gen_scores = (
        jnp.einsum(
            "btngd,bsnd->btngs", grouped, gen_block[:, :, 0], preferred_element_type=jnp.float32
        )
        * score_scale
    )
    new_scores = (
        jnp.einsum(
            "btngd,bsnd->btngs", grouped, new_block[:, :, 0], preferred_element_type=jnp.float32
        )
        * score_scale
    )
    causal = lax.broadcasted_iota(jnp.int32, (2, 2), 1) <= lax.broadcasted_iota(
        jnp.int32, (2, 2), 0
    )
    new_scores = jnp.where(causal[None, :, None, None, :], new_scores, -jnp.inf)
    row_max = jnp.maximum(
        jnp.maximum(prompt_scores.max(-1), gen_scores.max(-1)), new_scores.max(-1)
    )[..., None]
    prompt_exp = jnp.exp(prompt_scores - row_max)
    gen_exp = jnp.exp(gen_scores - row_max)
    new_exp = jnp.exp(new_scores - row_max)
    denom = (prompt_exp.sum(-1) + gen_exp.sum(-1) + new_exp.sum(-1))[..., None]
    prompt_weights = (prompt_exp / denom).astype(jnp.bfloat16)
    gen_weights = (gen_exp / denom).astype(jnp.bfloat16)
    new_weights = (new_exp / denom).astype(jnp.bfloat16)
    result = jnp.einsum(
        "btngs,snd->btngd", prompt_weights, prompt_cache[:, 1], preferred_element_type=jnp.float32
    )
    result = result + jnp.einsum(
        "btngs,bsnd->btngd", gen_weights, gen_block[:, :, 1], preferred_element_type=jnp.float32
    )
    result = result + jnp.einsum(
        "btngs,bsnd->btngd", new_weights, new_block[:, :, 1], preferred_element_type=jnp.float32
    )
    return result.reshape(count, 2, heads, head_dim).astype(jnp.bfloat16)


def slot_numbers(expert_ids, expert_count, capacity):
    flat_ids = expert_ids.reshape(-1)
    onehot = (flat_ids[:, None] == jnp.arange(expert_count, dtype=jnp.int32)[None, :]).astype(
        jnp.int32
    )
    before = jnp.cumsum(onehot, axis=0) - onehot
    rank = jnp.sum(before * onehot, axis=1)
    return (flat_ids * capacity + rank).reshape(expert_ids.shape)


def pack_rows(rows, slot_ids, slot_count):
    selector = (
        (jnp.arange(slot_count, dtype=jnp.int32)[:, None, None] == slot_ids[None, :, :])
        .any(-1)
        .astype(jnp.bfloat16)
    )
    return jnp.dot(selector, rows, preferred_element_type=jnp.float32).astype(jnp.bfloat16)


def shards(
    gen_cache,
    prompt_cache,
    ancestors,
    queries,
    new_kv,
    tokens_in,
    norm_gain,
    routes,
    gate_weights,
    w_gate_up,
    w_down,
):
    ep_count = lax.axis_size(EP)
    rep_count = lax.axis_size("rep")
    per_dev = gen_cache.shape[0]
    width = tokens_in.shape[2]
    top_count = routes.shape[3]
    parents = gather_axes(ancestors, (("ep_0", "ep_1"), "ep_2"), (0, 1), 0)
    piece_len = gen_cache.size // (per_dev * ep_count)
    flat_cache = gen_cache.reshape(per_dev, ep_count, piece_len)
    chosen = jnp.take(
        lax.all_to_all(flat_cache, EP, split_axis=1, concat_axis=0, tiled=True), parents, axis=0
    )
    moved = lax.all_to_all(chosen, EP, split_axis=0, concat_axis=1, tiled=True)
    cache_out = moved.reshape(gen_cache.shape)
    attn_out = attend(queries, cache_out, new_kv, prompt_cache)
    values_f = tokens_in.astype(jnp.float32).reshape(per_dev * 2, width)
    normed = (
        values_f
        * lax.rsqrt(jnp.mean(values_f * values_f, axis=-1, keepdims=True) + 1e-06)
        * norm_gain
    ).astype(jnp.bfloat16)
    half_cols = w_down.shape[1]
    weight_in = w_gate_up.reshape(width, 2 * half_cols)
    weight_out = w_down.reshape(half_cols, width)
    per_expert = min(2 * per_dev, 2 * ((2 * per_dev * top_count + ep_count - 1) // ep_count))
    rep_place = lax.axis_index("rep")
    own_routes = lax.dynamic_index_in_dim(routes, rep_place, 0, keepdims=False).reshape(
        -1, top_count
    )
    own_gates = lax.dynamic_index_in_dim(gate_weights, rep_place, 0, keepdims=False).reshape(
        -1, top_count
    )
    slot_ids = slot_numbers(own_routes, ep_count, per_expert)
    outgoing = pack_rows(normed, slot_ids, ep_count * per_expert).reshape(
        ep_count, per_expert, width
    )
    received = lax.all_to_all(outgoing, EP, split_axis=0, concat_axis=0, tiled=True)
    all_rows = lax.all_gather(received, "rep", axis=0, tiled=True)
    gate_up = jnp.dot(all_rows.reshape(-1, width), weight_in, preferred_element_type=jnp.float32)
    act = (jax.nn.silu(gate_up[:, :half_cols]) * gate_up[:, half_cols:]).astype(jnp.bfloat16)
    produced = (
        jnp.dot(act, weight_out, preferred_element_type=jnp.float32)
        .astype(jnp.bfloat16)
        .reshape(all_rows.shape)
    )
    parts_back = lax.all_to_all(produced, "rep", split_axis=0, concat_axis=0, tiled=True)
    added = jnp.sum(parts_back.astype(jnp.float32).reshape((rep_count,) + received.shape), axis=0)
    came_back = (
        lax.all_to_all(added.astype(jnp.bfloat16), EP, split_axis=0, concat_axis=0, tiled=True)
        .astype(added.dtype)
        .reshape(-1, width)
    )
    picked = jnp.take(came_back, slot_ids, axis=0)
    summed = jnp.sum(own_gates[:, :, None] * picked, axis=1)
    expert_out = summed.astype(jnp.bfloat16).reshape(per_dev, 2, width)
    return (cache_out, attn_out, expert_out)


def solution(mesh):
    torus = Mesh(mesh.devices.reshape(mesh.shape["rep"], 16, 4, 2), ("rep", "ep_0", "ep_1", "ep_2"))
    placed = (
        P(REP_EP, None, None, None, None),
        P(),
        P(REP_EP),
        P(REP_EP, None, None, None),
        P(REP_EP, None, None, None, None),
        P(REP_EP, None, None),
        P(),
        P(None, EP, None, None),
        P(None, EP, None, None),
        P(EP, None, None, "rep"),
        P(EP, "rep", None),
    )
    return jax.shard_map(
        shards,
        mesh=torus,
        in_specs=placed,
        out_specs=(
            P(REP_EP, None, None, None, None),
            P(REP_EP, None, None, None),
            P(REP_EP, None, None),
        ),
        check_vma=False,
    )
```

profile of v0, /device:TPU:33, one launch (start us, length us, event | category | flops | bytes accessed | tf_op | source)
XLA Modules:
  0.0 337.5 jit_solution(3306785641980755028)
XLA Ops:
  7.2 1.0 reshape.212
  8.2 1.0 multiply_reduce_fusion
  10.8 1.2 convolution_convert_fusion.1
  12.0 1.5 reshape.213
  13.5 75.1 %all_to_all.48 = bf16[128,2,2048]{2,1,0:T(2,128)(2,1)} all-to-all(bf16[128,2,2048]{2,1,0:T(2,128)(2,1)} %reshape.213), channel_id=1, replica_groups=mesh['rep'=4,'ep_0'=16,'ep_1'=4,'ep_2'=2] {'ep_0','ep_1','ep_2'}, dimensions={0} | all-to-all | bytes 2097152 | tf_op jit(solution)/shard_map/all_to_all | solution.py:151
  88.9 1.1 copy.143
  90.0 6.5 %all-to-all-start = ((bf16[8,128,256]{2,0,1:T(8,128)(2,1)}), bf16[8,128,256]{2,0,1:T(8,128)(2,1)S(1)}, u32[]{:S(2)}, u32[]{:S(2)}) async-start(bf16[8,128,256]{2,0,1:T(8,128)(2,1)} %copy.143), calls=%async_computation | async-start | bytes 1048576 | tf_op jit(solution)/shard_map/all_to_all | solution.py:125
  96.5 39.3 %all-gather.5.cloned.1.call-done = bf16[512,2,2048]{2,1,0:T(2,128)(2,1)} async-done(((bf16[128,2,2048]{2,1,0:T(2,128)(2,1)}), bf16[512,2,2048]{2,1,0:T(2,128)(2,1)}) %all-gather.5.cloned.1.call-update) | async-done | bytes 4194320 | tf_op jit(solution)/shard_map/all_gather | solution.py:152
  135.8 7.2 %reshape.214 = bf16[1024,2048]{1,0:T(8,128)(2,1)} reshape(bf16[512,2,2048]{2,1,0:T(2,128)(2,1)} %all-gather.5.cloned.1.call-done) | data formatting | bytes 8388608 | tf_op jit(solution)/shard_map/reshape | solution.py:153
  143.0 4.1 %fusion.32 = f32[1024,384]{0,1:T(8,128)S(1)} fusion(bf16[1024,2048]{1,0:T(8,128)(2,1)} %reshape.214, bf16[2048,384]{0,1:T(8,128)(2,1)S(1)} %bitcast.104), kind=kOutput, calls=%fused_computation.79 | convolution fusion | flops 1610612736 | bytes 7340032 | tf_op jit(solution)/shard_map/dot_general | solution.py:153
  147.1 3.3 convolution_convert_fusion
  150.4 7.6 %reshape.217 = bf16[512,2,2048]{2,1,0:T(2,128)(2,1)} reshape(bf16[1024,2048]{1,0:T(8,128)(2,1)} %convolution_convert_fusion) | data formatting | bytes 8388608 | tf_op jit(solution)/shard_map/reshape | solution.py:158
  158.0 5.0 %all-to-all-start.3 = ((bf16[512,2,2048]{2,1,0:T(2,128)(2,1)}), bf16[512,2,2048]{2,1,0:T(2,128)(2,1)}, u32[]{:S(2)}, u32[]{:S(2)}) async-start(bf16[512,2,2048]{2,1,0:T(2,128)(2,1)} %reshape.217), calls=%async_computation.3 | async-start | bytes 8388608 | tf_op jit(solution)/shard_map/all_to_all | solution.py:160
  163.0 1.3 dynamic-slice
  165.2 24.0 %all-reduce = s32[512]{0:T(512)S(1)} all-reduce(s32[512]{0:T(512)S(1)} %dynamic-update-slice), channel_id=2, replica_groups=mesh['rep'=4,'ep_0'=16,'ep_1'=4,'ep_2'=2] {'ep_0','ep_1'}, use_global_device_ids=true, to_apply=%add | all-reduce | flops 512 | bytes 4096
  189.3 6.6 %all-gather.2 = s32[2,64,8]{1,2,0:T(8,128)S(1)} all-gather(s32[1,64,8]{1,2,0:T(8,128)S(1)} %copy.141), channel_id=3, replica_groups=mesh['rep'=4,'ep_0'=16,'ep_1'=4,'ep_2'=2] {'ep_2'}, dimensions={0}, use_global_device_ids=true | all-gather | bytes 6144 | tf_op jit(solution)/shard_map/all_gather | solution.py:22
  196.4 3.9 %gather_fusion = bf16[1024,256]{1,0:T(8,128)(2,1)S(1)} fusion(bf16[1024,256]{1,0:T(8,128)(2,1)S(1)} %bitcast.105, s32[1024]{0:T(1024)S(1)} %broadcast_clamp_fusion), kind=kCustom, calls=%fused_computation | custom fusion | bytes 1052672 | tf_op jit(solution)/shard_map/jit(_take)/gather | solution.py:124
  201.1 1.0 reduce.2
  202.1 1.0 reshape.261
  203.1 8.0 %all-to-all-done.3 = bf16[512,2,2048]{2,1,0:T(2,128)(2,1)} async-done(((bf16[512,2,2048]{2,1,0:T(2,128)(2,1)}), bf16[512,2,2048]{2,1,0:T(2,128)(2,1)}, u32[]{:S(2)}, u32[]{:S(2)}) %all-to-all-start.3) | async-done | bytes 4194336 | tf_op jit(solution)/shard_map/all_to_all | solution.py:160
  211.1 17.9 %all-to-all-start.1 = ((bf16[128,2,1024]{2,1,0:T(2,128)(2,1)}), bf16[128,2,1024]{2,1,0:T(2,128)(2,1)S(1)}, u32[]{:S(2)}, u32[]{:S(2)}) async-start(bf16[128,2,1024]{2,1,0:T(2,128)(2,1)} %reshape.261), calls=%async_computation.1 | async-start | bytes 1048576 | tf_op jit(solution)/shard_map/all_to_all | solution.py:127
  229.0 8.2 %reduce.1 = bf16[128,2,2048]{2,1,0:T(2,128)(2,1)} reduce(bf16[4,128,2,2048]{3,2,1,0:T(2,128)(2,1)} %bitcast.38, bf16[]{:T(256)} %constant.80), dimensions={0}, to_apply=%region_10.11.clone | reduce | flops 1572864 | bytes 5242882 | tf_op jit(solution)/shard_map/reduce_sum | solution.py:161
  237.2 25.5 %all-to-all-done.1 = bf16[128,2,1024]{2,1,0:T(2,128)(2,1)S(1)} async-done(((bf16[128,2,1024]{2,1,0:T(2,128)(2,1)}), bf16[128,2,1024]{2,1,0:T(2,128)(2,1)S(1)}, u32[]{:S(2)}, u32[]{:S(2)}) %all-to-all-start.1) | async-done | bytes 524320 | tf_op jit(solution)/shard_map/all_to_all | solution.py:127
  262.7 6.2 %all-to-all-start.4 = ((bf16[128,2,2048]{2,1,0:T(2,128)(2,1)}), bf16[128,2,2048]{2,1,0:T(2,128)(2,1)S(1)}, u32[]{:S(2)}, u32[]{:S(2)}) async-start(bf16[128,2,2048]{2,1,0:T(2,128)(2,1)} %reduce.1), calls=%async_computation.4 | async-start | bytes 2097152 | tf_op jit(solution)/shard_map/all_to_all | solution.py:163
  271.2 1.9 fusion.27
  273.2 1.3 fusion.31
  274.5 1.8 reshape.262
  276.2 1.3 copy.229
  278.4 1.2 reshape.210
  284.0 40.5 %all-to-all-done.4 = bf16[128,2,2048]{2,1,0:T(2,128)(2,1)S(1)} async-done(((bf16[128,2,2048]{2,1,0:T(2,128)(2,1)}), bf16[128,2,2048]{2,1,0:T(2,128)(2,1)S(1)}, u32[]{:S(2)}, u32[]{:S(2)}) %all-to-all-start.4) | async-done | bytes 1048608 | tf_op jit(solution)/shard_map/all_to_all | solution.py:163
  324.5 1.5 reshape.223
  326.0 3.0 gather_fusion.1
  (72 shorter events, 12.6 us)
Async XLA Ops:
  7.2 135.8 %copy-start = (bf16[1,2048,2,192]{1,3,2,0:T(8,128)(2,1)S(1)}, bf16[1,2048,2,192]{1,3,2,0:T(8,128)(2,1)}, u32[]{:S(2)}) copy-start(bf16[1,2048,2,192]{1,3,2,0:T(8,128)(2,1)} %param.20) | copy-start | bytes 4718596
  7.2 128.6 %all-gather.5.cloned.1.call-start = ((), (), s32[]{:S(2)}) async-start(), calls=%async_computation.5 | async-start | bytes 5242880 | tf_op jit(solution)/shard_map/all_gather | solution.py:152
  13.5 75.1 %copy-start.4 = (bf16[8,32,2,4,128]{4,3,2,1,0:T(4,128)(2,1)S(1)}, bf16[8,32,2,4,128]{4,3,2,1,0:T(4,128)(2,1)}, u32[]{:S(2)}) copy-start(bf16[8,32,2,4,128]{4,3,2,1,0:T(4,128)(2,1)} %param.11) | copy-start | bytes 1572868
  90.0 68.0 %all-to-all-start = ((bf16[8,128,256]{2,0,1:T(8,128)(2,1)}), bf16[8,128,256]{2,0,1:T(8,128)(2,1)S(1)}, u32[]{:S(2)}, u32[]{:S(2)}) async-start(bf16[8,128,256]{2,0,1:T(8,128)(2,1)} %copy.143), calls=%async_computation | async-start | bytes 1048576 | tf_op jit(solution)/shard_map/all_to_all | solution.py:125
  143.0 4.1 %copy-start.8 = (bf16[1,192,2048]{2,1,0:T(8,128)(2,1)S(1)}, bf16[1,192,2048]{2,1,0:T(8,128)(2,1)}, u32[]{:S(2)}) copy-start(bf16[1,192,2048]{2,1,0:T(8,128)(2,1)} %param.21) | copy-start | bytes 2359300
  158.0 6.9 %copy-start.9 = (s32[8]{0:T(128)S(1)}, s32[8]{0:T(128)}, u32[]{:S(2)}) copy-start(s32[8]{0:T(128)} %param.13) | copy-start | bytes 100
  158.0 53.1 %all-to-all-start.3 = ((bf16[512,2,2048]{2,1,0:T(2,128)(2,1)}), bf16[512,2,2048]{2,1,0:T(2,128)(2,1)}, u32[]{:S(2)}, u32[]{:S(2)}) async-start(bf16[512,2,2048]{2,1,0:T(2,128)(2,1)} %reshape.217), calls=%async_computation.3 | async-start | bytes 8388608 | tf_op jit(solution)/shard_map/all_to_all | solution.py:160
  211.1 51.6 %all-to-all-start.1 = ((bf16[128,2,1024]{2,1,0:T(2,128)(2,1)}), bf16[128,2,1024]{2,1,0:T(2,128)(2,1)S(1)}, u32[]{:S(2)}, u32[]{:S(2)}) async-start(bf16[128,2,1024]{2,1,0:T(2,128)(2,1)} %reshape.261), calls=%async_computation.1 | async-start | bytes 1048576 | tf_op jit(solution)/shard_map/all_to_all | solution.py:127
  237.2 32.7 %copy-start.6 = (bf16[8,2,2,4,128]{4,3,2,1,0:T(4,128)(2,1)S(1)}, bf16[8,2,2,4,128]{4,3,2,1,0:T(4,128)(2,1)}, u32[]{:S(2)}) copy-start(bf16[8,2,2,4,128]{4,3,2,1,0:T(4,128)(2,1)} %param.15) | copy-start | bytes 98308
  237.2 33.3 %copy-start.3 = (bf16[8,2,64,128]{3,2,1,0:T(8,128)(2,1)S(1)}, bf16[8,2,64,128]{3,2,1,0:T(8,128)(2,1)}, u32[]{:S(2)}) copy-start(bf16[8,2,64,128]{3,2,1,0:T(8,128)(2,1)} %param.14) | copy-start | bytes 786436
  262.7 61.8 %all-to-all-start.4 = ((bf16[128,2,2048]{2,1,0:T(2,128)(2,1)}), bf16[128,2,2048]{2,1,0:T(2,128)(2,1)S(1)}, u32[]{:S(2)}, u32[]{:S(2)}) async-start(bf16[128,2,2048]{2,1,0:T(2,128)(2,1)} %reduce.1), calls=%async_computation.4 | async-start | bytes 2097152 | tf_op jit(solution)/shard_map/all_to_all | solution.py:163
  279.6 1.9 copy-start.2
  279.6 1.4 copy-start.1
  279.6 2.0 copy-start.5
  282.3 0.7 copy-start.7
Sparse Core Ops, SparseCore 0:
  88.7 47.0 all-gather.4
where the time goes:
time: 339 us; the launch traced here: 338 us
  waiting for transfers between devices  113 us (33%)
  blocking collectives  106 us (31%)
  local copies, waits for them, and re-layouts  41.5 us (12%)
  starting transfers between devices  35.6 us (11%)
  between operations  15.1 us (4%)
  other arithmetic  13.7 us (4%)
  matrix products  12.6 us (4%)
    all_to_all x1, blocking collectives, shards(): lax.all_to_all(outgoing, EP, split_axis=0, concat_axis=0, tiled=True)  75.1 us
    all_to_all x1, waiting for transfers between devices, shards(): lax.all_to_all(added.astype(jnp.bfloat16), EP, split_axis=0, concat_axis=...  40.5 us
    all_gather x1, waiting for transfers between devices, shards(): all_rows = lax.all_gather(received, 'rep', axis=0, tiled=True)  39.3 us
    all_to_all x1, waiting for transfers between devices, shards(): moved = lax.all_to_all(chosen, EP, split_axis=0, concat_axis=1, tiled=True)  25.5 us
    unnamed x1, blocking collectives  24 us
    all_to_all x1, starting transfers between devices, shards(): moved = lax.all_to_all(chosen, EP, split_axis=0, concat_axis=1, tiled=True)  17.9 us
    reduce_sum x1, other arithmetic, shards(): jnp.sum(parts_back.astype(jnp.float32).reshape((rep_count,) + received.sh...  8.18 us
    all_to_all x1, waiting for transfers between devices, shards(): lax.all_to_all(produced, 'rep', split_axis=0, concat_axis=0, tiled=True)  8.01 us
  transfers between devices with their start and end apart: 5, of which 4 were waited for; matrix products, arithmetic and copies ran while one was open for 16% of the time, Pallas kernels for 0%

commit v1 on v0

v1 whole, which is shorter than its diff:
```python
import math

import jax
import jax.numpy as jnp
from jax import lax
from jax.experimental import pallas as pl
from jax.experimental.pallas import tpu as pltpu
from jax.sharding import Mesh
from jax.sharding import PartitionSpec as P


EP = ("ep_0", "ep_1", "ep_2")
REP_EP = ("rep", "ep_0", "ep_1", "ep_2")


def shift(block, axis, count, step):
    return lax.ppermute(block, axis, [(i, (i + step) % count) for i in range(count)])


def ring_gather(block):
    half = block.shape[0] // 2
    before = shift(block, "rep", 4, 1)
    after = shift(block, "rep", 4, -1)
    far_low = shift(before[:half], "rep", 4, 1)
    far_high = shift(after[half:], "rep", 4, -1)
    return before, after, far_low, far_high


def ring_rows(block):
    wide = [block] + [shift(block, "ep_0", 16, step) for step in (4, -4, 8)]
    wide = jnp.concatenate(wide, axis=0)
    return [wide] + [shift(wide, "ep_0", 16, step) for step in (1, -1, 2)]


def select_body(place_ref, own_ref, back_ref, ahead_ref, far_ref, out_ref, rows_ref, *, width):
    for n, part in enumerate((own_ref, back_ref, ahead_ref, far_ref)):
        rows_ref[n * 64 : (n + 1) * 64, :] = part[...]
    count = rows_ref.shape[0]
    slots = out_ref.shape[0]
    place = place_ref[0]
    row = lax.broadcasted_iota(jnp.int32, (count, 1), 0)
    near, wide = row // 64, row // 16 % 4
    distance = jnp.where(near == 1, -1, jnp.where(near == 2, 1, jnp.where(near == 3, -2, 0)))
    distance += jnp.where(wide == 1, -4, jnp.where(wide == 2, 4, jnp.where(wide == 3, -8, 0)))
    source = (place + distance + 16) % 16
    column = lax.broadcasted_iota(jnp.int32, (count, slots), 1)
    expert = place * 8 + column // 32
    ids = rows_ref[:, width:].astype(jnp.int32)
    named = ids[:, 0:1] == expert
    for k in range(1, 8):
        named = named | (ids[:, k : k + 1] == expert)
    lower = lax.broadcasted_iota(jnp.int32, (count, count), 0)
    upper = lax.broadcasted_iota(jnp.int32, (count, count), 1)
    earlier = (upper < lower) & (upper // 16 == lower // 16)
    rank = jnp.dot(
        earlier.astype(jnp.float32).astype(jnp.bfloat16),
        named.astype(jnp.float32).astype(jnp.bfloat16),
        preferred_element_type=jnp.float32,
    ).astype(jnp.int32)
    chosen = named & (source * 2 + rank == column % 32)
    out_ref[...] = lax.dot_general(
        chosen.astype(jnp.float32).astype(jnp.bfloat16),
        rows_ref[:, :width],
        (((0,), (0,)), ((), ())),
        preferred_element_type=jnp.float32,
    ).astype(jnp.bfloat16)


def select_rows(place, blocks, width, slots):
    rows = sum(b.shape[0] for b in blocks)
    spec = pl.BlockSpec(memory_space=pltpu.VMEM)
    return pl.pallas_call(
        lambda *refs: select_body(*refs, width=width),
        out_shape=jax.ShapeDtypeStruct((slots, width), jnp.bfloat16),
        in_specs=[pl.BlockSpec(memory_space=pltpu.SMEM)] + [spec] * 4,
        out_specs=spec,
        scratch_shapes=[pltpu.VMEM((rows, blocks[0].shape[1]), jnp.bfloat16)],
        name="select_rows",
    )(place.reshape(1), *blocks)


def expert_body(
    rows_hbm, in_hbm, out_hbm, before_hbm, after_hbm, low_hbm, high_hbm, result_hbm,
    rows, own, before, after, far, result, sems,
):
    hidden = own.shape[0] // 3
    half = low_hbm.shape[0]
    copies = [
        pltpu.make_async_copy(src, dst, sems.at[n])
        for n, (src, dst) in enumerate(
            (
                (rows_hbm, rows),
                (in_hbm, own.at[: 2 * hidden]),
                (out_hbm, own.at[2 * hidden :]),
                (before_hbm, before),
                (after_hbm, after),
                (low_hbm, far.at[:half]),
                (high_hbm, far.at[half:]),
            )
        )
    ]
    for copy in copies:
        copy.start()
    count = rows.shape[0]
    to = lax.broadcasted_iota(jnp.int32, (count, count), 0)
    come = lax.broadcasted_iota(jnp.int32, (count, count), 1)
    order = come == to // 2 % 8 * 32 + to // 16 * 2 + to % 2
    order = order.astype(jnp.float32).astype(jnp.bfloat16)
    total = None
    contract = (((1,), (1,)), ((), ()))
    for weights, waits in ((own, (0, 1, 2)), (before, (3,)), (after, (4,)), (far, (5, 6))):
        for n in waits:
            copies[n].wait()
        both = lax.dot_general(
            rows[...], weights[: 2 * hidden], contract, preferred_element_type=jnp.float32
        )
        gate, upward = both[:, :hidden], both[:, hidden:]
        act = (gate / (1.0 + jnp.exp(-gate)) * upward).astype(jnp.bfloat16)
        act = jnp.dot(order, act, preferred_element_type=jnp.float32).astype(jnp.bfloat16)
        part = jnp.dot(act, weights[2 * hidden :], preferred_element_type=jnp.float32)
        total = part if total is None else total + part
    result[...] = total.astype(jnp.bfloat16)
    last = pltpu.make_async_copy(result, result_hbm, sems.at[7])
    last.start()
    last.wait()


def expert(rows, in_own, out_own, before, after, low, high):
    count, width = rows.shape
    span = before.shape[0]
    return pl.pallas_call(
        expert_body,
        out_shape=jax.ShapeDtypeStruct((count, width), jnp.bfloat16),
        in_specs=[pl.BlockSpec(memory_space=pl.ANY)] * 7,
        out_specs=pl.BlockSpec(memory_space=pl.ANY),
        scratch_shapes=[pltpu.VMEM((count, width), jnp.bfloat16)]
        + [pltpu.VMEM((span, width), jnp.bfloat16)] * 4
        + [pltpu.VMEM((count, width), jnp.bfloat16), pltpu.SemaphoreType.DMA((8,))],
        compiler_params=pltpu.CompilerParams(vmem_limit_bytes=32 * 1024 * 1024),
        name="expert",
    )(rows, in_own, out_own, before, after, low, high)


def attend(queries, gen_block, new_block, prompt_cache):
    count = queries.shape[0]
    heads = queries.shape[2]
    head_dim = queries.shape[3]
    kv_heads = new_block.shape[3]
    score_scale = 1.0 / math.sqrt(head_dim)
    grouped = queries.reshape(count, 2, kv_heads, heads // kv_heads, head_dim)
    prompt_scores = (
        jnp.einsum(
            "btngd,snd->btngs", grouped, prompt_cache[:, 0], preferred_element_type=jnp.float32
        )
        * score_scale
    )
    gen_scores = (
        jnp.einsum(
            "btngd,bsnd->btngs", grouped, gen_block[:, :, 0], preferred_element_type=jnp.float32
        )
        * score_scale
    )
    new_scores = (
        jnp.einsum(
            "btngd,bsnd->btngs", grouped, new_block[:, :, 0], preferred_element_type=jnp.float32
        )
        * score_scale
    )
    causal = lax.broadcasted_iota(jnp.int32, (2, 2), 1) <= lax.broadcasted_iota(
        jnp.int32, (2, 2), 0
    )
    new_scores = jnp.where(causal[None, :, None, None, :], new_scores, -jnp.inf)
    row_max = jnp.maximum(
        jnp.maximum(prompt_scores.max(-1), gen_scores.max(-1)), new_scores.max(-1)
    )[..., None]
    prompt_exp = jnp.exp(prompt_scores - row_max)
    gen_exp = jnp.exp(gen_scores - row_max)
    new_exp = jnp.exp(new_scores - row_max)
    denom = (prompt_exp.sum(-1) + gen_exp.sum(-1) + new_exp.sum(-1))[..., None]
    prompt_weights = (prompt_exp / denom).astype(jnp.bfloat16)
    gen_weights = (gen_exp / denom).astype(jnp.bfloat16)
    new_weights = (new_exp / denom).astype(jnp.bfloat16)
    result = jnp.einsum(
        "btngs,snd->btngd", prompt_weights, prompt_cache[:, 1], preferred_element_type=jnp.float32
    )
    result = result + jnp.einsum(
        "btngs,bsnd->btngd", gen_weights, gen_block[:, :, 1], preferred_element_type=jnp.float32
    )
    result = result + jnp.einsum(
        "btngs,bsnd->btngd", new_weights, new_block[:, :, 1], preferred_element_type=jnp.float32
    )
    return result.reshape(count, 2, heads, head_dim).astype(jnp.bfloat16)


def slot_numbers(expert_ids, capacity):
    flat_ids = expert_ids.reshape(-1)
    count = flat_ids.shape[0]
    earlier = lax.broadcasted_iota(jnp.int32, (count, count), 1) < lax.broadcasted_iota(
        jnp.int32, (count, count), 0
    )
    same = (flat_ids[:, None] == flat_ids[None, :]) & earlier
    rank = jnp.sum(same.astype(jnp.int32), axis=1)
    return (flat_ids * capacity + rank).reshape(expert_ids.shape)


def shards(
    gen_cache,
    prompt_cache,
    ancestors,
    queries,
    new_kv,
    tokens_in,
    norm_gain,
    routes,
    gate_weights,
    w_gate_up,
    w_down,
):
    ep_count = lax.axis_size(EP)
    per_dev = gen_cache.shape[0]
    row_count = 2 * per_dev
    width = tokens_in.shape[2]
    top_count = routes.shape[3]
    half_cols = w_down.shape[1]
    per_expert = 2
    slot_count = ep_count * per_expert

    in_own = w_gate_up.reshape(width, 2 * half_cols).T
    out_own = w_down.reshape(half_cols, width)
    before, after, low, high = ring_gather(jnp.concatenate([in_own, out_own], axis=0))

    piece_len = gen_cache.size // (per_dev * ep_count)
    flat_cache = (
        gen_cache.reshape(per_dev, ep_count, piece_len)
        .transpose(1, 0, 2)
        .reshape(ep_count, 2, per_dev * piece_len // 2)
    )
    flat_len = flat_cache.shape[2]
    digits = jnp.concatenate([ancestors // 256, ancestors % 256]).astype(jnp.bfloat16)
    side = jnp.pad(digits, (0, 128 - digits.shape[0]))
    flat_cache = jnp.concatenate(
        [flat_cache, jnp.broadcast_to(side, (ep_count, 2, side.shape[0]))], axis=2
    )
    pieces = lax.all_to_all(flat_cache, EP, split_axis=0, concat_axis=0, tiled=True)
    tail = pieces[:, 0, flat_len : flat_len + 2 * per_dev].astype(jnp.int32)
    parents = (tail[:, :per_dev] * 256 + tail[:, per_dev:]).reshape(-1)
    pieces = pieces[:, :, :flat_len].reshape(-1, piece_len)
    chosen = jnp.take(pieces, parents, axis=0, mode="clip").reshape(ep_count, 2, flat_len)
    moved = lax.all_to_all(chosen, EP, split_axis=0, concat_axis=0, tiled=True)
    cache_out = (
        moved.reshape(ep_count, per_dev, piece_len).transpose(1, 0, 2).reshape(gen_cache.shape)
    )
    attn_out = attend(queries, cache_out, new_kv, prompt_cache)

    values_f = tokens_in.astype(jnp.float32).reshape(row_count, width)
    normed = (
        values_f
        * lax.rsqrt(jnp.mean(values_f * values_f, axis=-1, keepdims=True) + 1e-06)
        * norm_gain
    ).astype(jnp.bfloat16)
    rep_place = lax.axis_index("rep")
    own_routes = lax.dynamic_index_in_dim(routes, rep_place, 0, keepdims=False).reshape(
        -1, top_count
    )
    own_gates = lax.dynamic_index_in_dim(gate_weights, rep_place, 0, keepdims=False).reshape(
        -1, top_count
    )
    labels = jnp.pad(own_routes.astype(jnp.bfloat16), ((0, 0), (0, 128 - top_count)))
    blocks = ring_rows(jnp.concatenate([normed, labels], axis=1))
    planes = lax.axis_size("ep_0")
    local = ep_count // planes
    packed = select_rows(lax.axis_index("ep_0"), blocks, width, slot_count)
    rows = lax.all_to_all(
        packed.reshape(local, planes * per_expert, width),
        EP[1:],
        split_axis=0,
        concat_axis=0,
        tiled=True,
    ).reshape(slot_count, width)
    produced = expert(rows, in_own, out_own, before, after, low, high)
    produced = produced.reshape(ep_count, per_expert, width)

    slot_ids = slot_numbers(own_routes, per_expert)
    hits = jnp.arange(slot_count, dtype=jnp.int32)[:, None, None] == slot_ids[None, :, :]
    gate_of_slot = jnp.sum(jnp.where(hits, own_gates[None, :, :], 0.0), axis=-1).T
    came_back = lax.all_to_all(produced, EP, split_axis=0, concat_axis=0, tiled=True)
    came_back = came_back.reshape(slot_count, width)
    summed = jnp.dot(
        gate_of_slot,
        came_back.astype(jnp.float32),
        precision=lax.Precision.HIGHEST,
        preferred_element_type=jnp.float32,
    )
    expert_out = summed.astype(jnp.bfloat16).reshape(per_dev, 2, width)
    return (cache_out, attn_out, expert_out)


def solution(mesh):
    torus = Mesh(mesh.devices.reshape(mesh.shape["rep"], 16, 4, 2), ("rep", "ep_0", "ep_1", "ep_2"))
    placed = (
        P(REP_EP, None, None, None, None),
        P(),
        P(REP_EP),
        P(REP_EP, None, None, None),
        P(REP_EP, None, None, None, None),
        P(REP_EP, None, None),
        P(),
        P(None, EP, None, None),
        P(None, EP, None, None),
        P(EP, None, None, "rep"),
        P(EP, "rep", None),
    )
    return jax.shard_map(
        shards,
        mesh=torus,
        in_specs=placed,
        out_specs=(
            P(REP_EP, None, None, None, None),
            P(REP_EP, None, None, None),
            P(REP_EP, None, None),
        ),
        check_vma=False,
    )
```

time: 339 us -> 247 us (0.73)
  the two profiles are of different devices: /device:TPU:33 before, /device:TPU:41 now
where the time goes in v1:
time: 247 us; the launch traced here: 246 us
  waiting for transfers between devices  109 us (44%)
  starting transfers between devices  88 us (36%)
  local copies, waits for them, and re-layouts  27.3 us (11%)
  Pallas kernels  9.69 us (4%)
  other arithmetic  7.1 us (3%)
  matrix products  3.72 us (2%)
    ppermute x10, waiting for transfers between devices, shift(): lax.ppermute(block, axis, [(i, (i + step) % count) for i in range(count)])  59.3 us
    all_to_all x1, waiting for transfers between devices, shards(): lax.all_to_all(produced, EP, split_axis=0, concat_axis=0, tiled=True)  45.6 us
    ppermute x10, starting transfers between devices, shift(): lax.ppermute(block, axis, [(i, (i + step) % count) for i in range(count)])  38.4 us
    all_to_all x1, starting transfers between devices, shards(): lax.all_to_all(flat_cache, EP, split_axis=0, concat_axis=0, tiled=True)  19.3 us
    all_to_all x1, starting transfers between devices, shards(): lax.all_to_all(produced, EP, split_axis=0, concat_axis=0, tiled=True)  17.3 us
    all_to_all x1, starting transfers between devices, shards(): moved = lax.all_to_all(chosen, EP, split_axis=0, concat_axis=0, tiled=True)  7.56 us
    pallas_call x1, Pallas kernels, expert(): pl.pallas_call(expert_body, out_shape=jax.ShapeDtypeStruct((count, width)...  6.33 us
    all_to_all x1, starting transfers between devices, shards(): lax.all_to_all(packed.reshape(local, planes * per_expert, width), EP[1:],...  5.42 us
  transfers between devices with their start and end apart: 14, of which 10 were waited for; matrix products, arithmetic and copies ran while one was open for 12% of the time, Pallas kernels for 4%

profile of v1, /device:TPU:41, one launch (start us, length us, event | category | flops | bytes accessed | tf_op | source)
XLA Modules:
  0.0 246.2 jit_solution(8158569960249424771)
XLA Ops:
  5.1 1.8 copy.154
  6.9 19.3 %all-to-all-start = ((bf16[128,2,1152]{2,1,0:T(2,128)(2,1)}), bf16[128,2,1152]{2,1,0:T(2,128)(2,1)S(1)}, u32[]{:S(2)}, u32[]{:S(2)}) async-start(bf16[128,2,1152]{2,1,0:T(2,128)(2,1)} %copy.154), calls=%async_computation | async-start | bytes 1179648 | tf_op jit(solution)/shard_map/all_to_all | solution.py:244
  27.3 7.2 %collective-permute-start = (bf16[16,2176]{1,0:T(8,128)(2,1)S(1)}, bf16[16,2176]{1,0:T(8,128)(2,1)S(1)}, u32[]{:S(2)}, u32[]{:S(2)}) collective-permute-start(bf16[16,2176]{1,0:T(8,128)(2,1)S(1)} %pad_maximum_fusion.3), channel_id=1, source_target_pairs={{0,32},{8,40},{16,48},{24,56},{32,64},{40,72},{48,80},{56,88},{64,... | collective-permute-start | bytes 208904 | tf_op jit(solution)/shard_map/ppermute | solution.py:17
  34.5 2.0 collective-permute-start.1
  36.5 11.3 %collective-permute-start.2 = (bf16[16,2176]{1,0:T(8,128)(2,1)S(1)}, bf16[16,2176]{1,0:T(8,128)(2,1)S(1)}, u32[]{:S(2)}, u32[]{:S(2)}) collective-permute-start(bf16[16,2176]{1,0:T(8,128)(2,1)S(1)} %pad_maximum_fusion.3), channel_id=1, source_target_pairs={{0,64},{8,72},{16,80},{24,88},{32,96},{40,104},{48,112},{56,120},{... | collective-permute-start | bytes 208904 | tf_op jit(solution)/shard_map/ppermute | solution.py:17
  47.8 1.7 pad_maximum_fusion
  49.5 3.2 %collective-permute-start.6 = (bf16[576,2048]{1,0:T(8,128)(2,1)}, bf16[576,2048]{1,0:T(8,128)(2,1)}, u32[]{:S(2)}, u32[]{:S(2)}) collective-permute-start(bf16[576,2048]{1,0:T(8,128)(2,1)} %pad_maximum_fusion), channel_id=1, source_target_pairs={{0,128},{128,256},{256,384},{384,0},{1,129},{129,257},{257,385},{3... | collective-permute-start | bytes 7077896 | tf_op jit(solution)/shard_map/ppermute | solution.py:17
  52.7 2.1 collective-permute-start.7
  54.8 4.8 %collective-permute-done = bf16[16,2176]{1,0:T(8,128)(2,1)S(1)} collective-permute-done((bf16[16,2176]{1,0:T(8,128)(2,1)S(1)}, bf16[16,2176]{1,0:T(8,128)(2,1)S(1)}, u32[]{:S(2)}, u32[]{:S(2)}) %collective-permute-start) | collective-permute-done | bytes 69664 | tf_op jit(solution)/shard_map/ppermute | solution.py:17
  59.6 2.2 collective-permute-done.1
  61.8 9.5 %collective-permute-done.2 = bf16[16,2176]{1,0:T(8,128)(2,1)S(1)} collective-permute-done((bf16[16,2176]{1,0:T(8,128)(2,1)S(1)}, bf16[16,2176]{1,0:T(8,128)(2,1)S(1)}, u32[]{:S(2)}, u32[]{:S(2)}) %collective-permute-start.2) | collective-permute-done | bytes 69664 | tf_op jit(solution)/shard_map/ppermute | solution.py:17
  71.4 1.9 collective-permute-start.3
  73.3 3.4 %collective-permute-start.4 = (bf16[64,2176]{1,0:T(8,128)(2,1)S(1)}, bf16[64,2176]{1,0:T(8,128)(2,1)S(1)}, u32[]{:S(2)}, u32[]{:S(2)}) collective-permute-start(bf16[64,2176]{1,0:T(8,128)(2,1)S(1)} %pad_maximum_fusion.2.refs_1_), channel_id=1, source_target_pairs={{0,120},{8,0},{16,8},{24,16},{32,24},{40,32},{48,40},{56,48},{64,5... | collective-permute-start | bytes 835592 | tf_op jit(solution)/shard_map/ppermute | solution.py:17
  76.7 1.9 collective-permute-start.5
  79.9 2.2 collective-permute-done.4.refs_3_
  82.1 12.8 %collective-permute-done.5.refs_4_ = bf16[64,2176]{1,0:T(8,128)(2,1)S(1)} collective-permute-done((bf16[64,2176]{1,0:T(8,128)(2,1)S(1)}, bf16[64,2176]{1,0:T(8,128)(2,1)S(1)}, u32[]{:S(2)}, u32[]{:S(2)}) %collective-permute-start.5) | collective-permute-done | bytes 278560 | tf_op jit(solution)/shard_map/ppermute | solution.py:17
  95.6 3.4 %select_rows.1 = bf16[256,2048]{1,0:T(8,128)(2,1)} custom-call(s32[1]{0:T(128)} %bitcast.33.refs_0_, bf16[64,2176]{1,0:T(8,128)(2,1)} %copy-done.8, bf16[64,2176]{1,0:T(8,128)(2,1)} %copy-done.10, bf16[64,2176]{1,0:T(8,128)(2,1)} %copy-done.11, bf16[64,2176]{1,0:T(8,128)(2,1)} %copy-done.12), custom_call_target="tpu_custom_call" | custom-call | tf_op jit(solution)/shard_map/select_rows/pallas_call | solution.py:72
  99.0 5.4 %all-to-all-start.2 = ((bf16[8,32,2048]{2,1,0:T(8,128)(2,1)}), bf16[8,32,2048]{2,1,0:T(8,128)(2,1)S(1)}, u32[]{:S(2)}, u32[]{:S(2)}) async-start(bf16[8,32,2048]{2,1,0:T(8,128)(2,1)} %bitcast.92), calls=%async_computation.2 | async-start | bytes 2097152 | tf_op jit(solution)/shard_map/all_to_all | solution.py:273
  107.9 5.0 %gather_fusion = bf16[1024,256]{1,0:T(8,128)(2,1)} fusion(bf16[1024,256]{1,0:T(8,128)(2,1)S(1)} %reshape.125, s32[1024]{0:T(1024)S(1)} %broadcast_clamp_fusion), kind=kCustom, calls=%fused_computation | custom fusion | bytes 1052672 | tf_op jit(solution)/shard_map/jit(_take)/gather | solution.py:248
  112.9 2.1 reshape.126
  114.9 4.4 %all-to-all-done.2 = bf16[8,32,2048]{2,1,0:T(8,128)(2,1)S(1)} async-done(((bf16[8,32,2048]{2,1,0:T(8,128)(2,1)}), bf16[8,32,2048]{2,1,0:T(8,128)(2,1)S(1)}, u32[]{:S(2)}, u32[]{:S(2)}) %all-to-all-start.2) | async-done | bytes 1048608 | tf_op jit(solution)/shard_map/all_to_all | solution.py:273
  119.3 7.6 %all-to-all-start.1 = ((bf16[128,2,1024]{2,1,0:T(2,128)(2,1)}), bf16[128,2,1024]{2,1,0:T(2,128)(2,1)S(1)}, u32[]{:S(2)}, u32[]{:S(2)}) async-start(bf16[128,2,1024]{2,1,0:T(2,128)(2,1)} %reshape.126), calls=%async_computation.1 | async-start | bytes 1048576 | tf_op jit(solution)/shard_map/all_to_all | solution.py:249
  126.9 1.5 slice.56
  128.4 3.2 %collective-permute-start.8 = (bf16[288,2048]{1,0:T(8,128)(2,1)S(1)}, bf16[288,2048]{1,0:T(8,128)(2,1)S(1)}, u32[]{:S(2)}, u32[]{:S(2)}) collective-permute-start(bf16[288,2048]{1,0:T(8,128)(2,1)S(1)} %slice.56), channel_id=1, source_target_pairs={{0,128},{128,256},{256,384},{384,0},{1,129},{129,257},{257,385},{3... | collective-permute-start | bytes 3538952 | tf_op jit(solution)/shard_map/ppermute | solution.py:17
  131.6 1.4 slice.57
  133.0 2.3 collective-permute-start.9
  135.3 22.1 %collective-permute-done.8.low_hbm = bf16[288,2048]{1,0:T(8,128)(2,1)S(1)} collective-permute-done((bf16[288,2048]{1,0:T(8,128)(2,1)S(1)}, bf16[288,2048]{1,0:T(8,128)(2,1)S(1)}, u32[]{:S(2)}, u32[]{:S(2)}) %collective-permute-start.8) | collective-permute-done | bytes 1179680 | tf_op jit(solution)/shard_map/ppermute | solution.py:17
  157.4 4.3 %collective-permute-done.9.high_hbm = bf16[288,2048]{1,0:T(8,128)(2,1)S(1)} collective-permute-done((bf16[288,2048]{1,0:T(8,128)(2,1)S(1)}, bf16[288,2048]{1,0:T(8,128)(2,1)S(1)}, u32[]{:S(2)}, u32[]{:S(2)}) %collective-permute-start.9) | collective-permute-done | bytes 1179680 | tf_op jit(solution)/shard_map/ppermute | solution.py:17
  161.8 6.3 %expert.1 = bf16[256,2048]{1,0:T(8,128)(2,1)S(1)} custom-call(bf16[256,2048]{1,0:T(8,128)(2,1)S(1)} %bitcast.89, bf16[384,2048]{1,0:T(8,128)(2,1)S(1)} %bitcast.88, bf16[192,2048]{1,0:T(8,128)(2,1)S(1)} %bitcast.91, bf16[576,2048]{1,0:T(8,128)(2,1)} %collective-permute-done.6.before_hbm, bf16[576,2048]{1,0:T(8,128)(2,1)} %collective-permute-done.7.after_hbm, ...), custom_call_target="tpu_custom_call" | custom-call | tf_op jit(solution)/shard_map/expert/pallas_call | solution.py:131
  169.1 2.6 %reshape.136 = bf16[128,2,2048]{2,1,0:T(2,128)(2,1)} reshape(bf16[256,2048]{1,0:T(8,128)(2,1)} %copy-done.2) | data formatting | bytes 2097152 | tf_op jit(solution)/shard_map/reshape | solution.py:281
  171.7 17.3 %all-to-all-start.3 = ((bf16[128,2,2048]{2,1,0:T(2,128)(2,1)}), bf16[128,2,2048]{2,1,0:T(2,128)(2,1)S(1)}, u32[]{:S(2)}, u32[]{:S(2)}) async-start(bf16[128,2,2048]{2,1,0:T(2,128)(2,1)} %reshape.136), calls=%async_computation.3 | async-start | bytes 2097152 | tf_op jit(solution)/shard_map/all_to_all | solution.py:286
  199.0 45.6 %all-to-all-done.3 = bf16[128,2,2048]{2,1,0:T(2,128)(2,1)S(1)} async-done(((bf16[128,2,2048]{2,1,0:T(2,128)(2,1)}), bf16[128,2,2048]{2,1,0:T(2,128)(2,1)S(1)}, u32[]{:S(2)}, u32[]{:S(2)}) %all-to-all-start.3) | async-done | bytes 1048608 | tf_op jit(solution)/shard_map/all_to_all | solution.py:286
  (95 shorter events, 23.4 us)
Async XLA Ops:
  0.6 190.3 %copy-start = (bf16[8,2,64,128]{3,2,1,0:T(8,128)(2,1)S(1)}, bf16[8,2,64,128]{3,2,1,0:T(8,128)(2,1)}, u32[]{:S(2)}) copy-start(bf16[8,2,64,128]{3,2,1,0:T(8,128)(2,1)} %param.14) | copy-start | bytes 786436
  2.7 23.5 %copy-start.13 = (bf16[8,2,2048]{2,1,0:T(2,128)(2,1)S(1)}, bf16[8,2,2048]{2,1,0:T(2,128)(2,1)}, u32[]{:S(2)}) copy-start(bf16[8,2,2048]{2,1,0:T(2,128)(2,1)} %param.16) | copy-start | bytes 196612
  2.7 24.4 %copy-start.17 = (f32[2048]{0:T(1024)S(1)}, f32[2048]{0:T(1024)}, u32[]{:S(2)}) copy-start(f32[2048]{0:T(1024)} %param.17) | copy-start | bytes 24580
  2.8 45.0 %copy-start.1 = (bf16[1,2048,2,192]{1,3,2,0:T(8,128)(2,1)S(1)}, bf16[1,2048,2,192]{1,3,2,0:T(8,128)(2,1)}, u32[]{:S(2)}) copy-start(bf16[1,2048,2,192]{1,3,2,0:T(8,128)(2,1)} %param.20) | copy-start | bytes 4718596
  2.8 45.0 %copy-start.3 = (bf16[1,192,2048]{2,1,0:T(8,128)(2,1)S(1)}, bf16[1,192,2048]{2,1,0:T(8,128)(2,1)}, u32[]{:S(2)}) copy-start(bf16[1,192,2048]{2,1,0:T(8,128)(2,1)} %param.21) | copy-start | bytes 2359300
  6.9 92.1 %all-to-all-start = ((bf16[128,2,1152]{2,1,0:T(2,128)(2,1)}), bf16[128,2,1152]{2,1,0:T(2,128)(2,1)S(1)}, u32[]{:S(2)}, u32[]{:S(2)}) async-start(bf16[128,2,1152]{2,1,0:T(2,128)(2,1)} %copy.154), calls=%async_computation | async-start | bytes 1179648 | tf_op jit(solution)/shard_map/all_to_all | solution.py:244
  27.3 32.3 %collective-permute-start = (bf16[16,2176]{1,0:T(8,128)(2,1)S(1)}, bf16[16,2176]{1,0:T(8,128)(2,1)S(1)}, u32[]{:S(2)}, u32[]{:S(2)}) collective-permute-start(bf16[16,2176]{1,0:T(8,128)(2,1)S(1)} %pad_maximum_fusion.3), channel_id=1, source_target_pairs={{0,32},{8,40},{16,48},{24,56},{32,64},{40,72},{48,80},{56,88},{64,... | collective-permute-start | bytes 208904 | tf_op jit(solution)/shard_map/ppermute | solution.py:17
  34.5 27.4 %collective-permute-start.1 = (bf16[16,2176]{1,0:T(8,128)(2,1)S(1)}, bf16[16,2176]{1,0:T(8,128)(2,1)S(1)}, u32[]{:S(2)}, u32[]{:S(2)}) collective-permute-start(bf16[16,2176]{1,0:T(8,128)(2,1)S(1)} %pad_maximum_fusion.3), channel_id=1, source_target_pairs={{0,96},{8,104},{16,112},{24,120},{32,0},{40,8},{48,16},{56,24},{64... | collective-permute-start | bytes 208904 | tf_op jit(solution)/shard_map/ppermute | solution.py:17
  36.5 34.9 %collective-permute-start.2 = (bf16[16,2176]{1,0:T(8,128)(2,1)S(1)}, bf16[16,2176]{1,0:T(8,128)(2,1)S(1)}, u32[]{:S(2)}, u32[]{:S(2)}) collective-permute-start(bf16[16,2176]{1,0:T(8,128)(2,1)S(1)} %pad_maximum_fusion.3), channel_id=1, source_target_pairs={{0,64},{8,72},{16,80},{24,88},{32,96},{40,104},{48,112},{56,120},{... | collective-permute-start | bytes 208904 | tf_op jit(solution)/shard_map/ppermute | solution.py:17
  49.5 77.4 %collective-permute-start.6 = (bf16[576,2048]{1,0:T(8,128)(2,1)}, bf16[576,2048]{1,0:T(8,128)(2,1)}, u32[]{:S(2)}, u32[]{:S(2)}) collective-permute-start(bf16[576,2048]{1,0:T(8,128)(2,1)} %pad_maximum_fusion), channel_id=1, source_target_pairs={{0,128},{128,256},{256,384},{384,0},{1,129},{129,257},{257,385},{3... | collective-permute-start | bytes 7077896 | tf_op jit(solution)/shard_map/ppermute | solution.py:17
  52.7 78.9 %collective-permute-start.7 = (bf16[576,2048]{1,0:T(8,128)(2,1)}, bf16[576,2048]{1,0:T(8,128)(2,1)}, u32[]{:S(2)}, u32[]{:S(2)}) collective-permute-start(bf16[576,2048]{1,0:T(8,128)(2,1)} %pad_maximum_fusion), channel_id=1, source_target_pairs={{0,384},{128,0},{256,128},{384,256},{1,385},{129,1},{257,129},{385... | collective-permute-start | bytes 7077896 | tf_op jit(solution)/shard_map/ppermute | solution.py:17
  71.4 23.5 %copy-start.8 = (bf16[64,2176]{1,0:T(8,128)(2,1)}, bf16[64,2176]{1,0:T(8,128)(2,1)S(1)}, u32[]{:S(2)}) copy-start(bf16[64,2176]{1,0:T(8,128)(2,1)S(1)} %pad_maximum_fusion.2.refs_1_) | copy-start | bytes 835588
  71.4 8.5 %collective-permute-start.3 = (bf16[64,2176]{1,0:T(8,128)(2,1)S(1)}, bf16[64,2176]{1,0:T(8,128)(2,1)S(1)}, u32[]{:S(2)}, u32[]{:S(2)}) collective-permute-start(bf16[64,2176]{1,0:T(8,128)(2,1)S(1)} %pad_maximum_fusion.2.refs_1_), channel_id=1, source_target_pairs={{0,8},{8,16},{16,24},{24,32},{32,40},{40,48},{48,56},{56,64},{64,7... | collective-permute-start | bytes 835592 | tf_op jit(solution)/shard_map/ppermute | solution.py:17
  73.3 8.8 %collective-permute-start.4 = (bf16[64,2176]{1,0:T(8,128)(2,1)S(1)}, bf16[64,2176]{1,0:T(8,128)(2,1)S(1)}, u32[]{:S(2)}, u32[]{:S(2)}) collective-permute-start(bf16[64,2176]{1,0:T(8,128)(2,1)S(1)} %pad_maximum_fusion.2.refs_1_), channel_id=1, source_target_pairs={{0,120},{8,0},{16,8},{24,16},{32,24},{40,32},{48,40},{56,48},{64,5... | collective-permute-start | bytes 835592 | tf_op jit(solution)/shard_map/ppermute | solution.py:17
  76.7 18.2 %collective-permute-start.5 = (bf16[64,2176]{1,0:T(8,128)(2,1)S(1)}, bf16[64,2176]{1,0:T(8,128)(2,1)S(1)}, u32[]{:S(2)}, u32[]{:S(2)}) collective-permute-start(bf16[64,2176]{1,0:T(8,128)(2,1)S(1)} %pad_maximum_fusion.2.refs_1_), channel_id=1, source_target_pairs={{0,16},{8,24},{16,32},{24,40},{32,48},{40,56},{48,64},{56,72},{64,... | collective-permute-start | bytes 835592 | tf_op jit(solution)/shard_map/ppermute | solution.py:17
  79.9 15.0 %copy-start.10 = (bf16[64,2176]{1,0:T(8,128)(2,1)}, bf16[64,2176]{1,0:T(8,128)(2,1)S(1)}, u32[]{:S(2)}) copy-start(bf16[64,2176]{1,0:T(8,128)(2,1)S(1)} %collective-permute-done.3.refs_2_) | copy-start | bytes 835588
  82.1 12.8 %copy-start.11 = (bf16[64,2176]{1,0:T(8,128)(2,1)}, bf16[64,2176]{1,0:T(8,128)(2,1)S(1)}, u32[]{:S(2)}) copy-start(bf16[64,2176]{1,0:T(8,128)(2,1)S(1)} %collective-permute-done.4.refs_3_) | copy-start | bytes 835588
  94.9 0.7 copy-start.12
  98.9 5.4 %copy-start.5 = (bf16[128,2,1152]{2,1,0:T(2,128)(2,1)}, bf16[128,2,1152]{2,1,0:T(2,128)(2,1)S(1)}, u32[]{:S(2)}) copy-start(bf16[128,2,1152]{2,1,0:T(2,128)(2,1)S(1)} %all-to-all-done) | copy-start | bytes 1769476
  99.0 20.4 %all-to-all-start.2 = ((bf16[8,32,2048]{2,1,0:T(8,128)(2,1)}), bf16[8,32,2048]{2,1,0:T(8,128)(2,1)S(1)}, u32[]{:S(2)}, u32[]{:S(2)}) async-start(bf16[8,32,2048]{2,1,0:T(8,128)(2,1)} %bitcast.92), calls=%async_computation.2 | async-start | bytes 2097152 | tf_op jit(solution)/shard_map/all_to_all | solution.py:273
  119.3 52.4 %all-to-all-start.1 = ((bf16[128,2,1024]{2,1,0:T(2,128)(2,1)}), bf16[128,2,1024]{2,1,0:T(2,128)(2,1)S(1)}, u32[]{:S(2)}, u32[]{:S(2)}) async-start(bf16[128,2,1024]{2,1,0:T(2,128)(2,1)} %reshape.126), calls=%async_computation.1 | async-start | bytes 1048576 | tf_op jit(solution)/shard_map/all_to_all | solution.py:249
  126.9 34.9 %copy-start.4 = (bf16[1,192,2048]{2,1,0:T(8,128)(2,1)S(1)}, bf16[1,192,2048]{2,1,0:T(8,128)(2,1)}, u32[]{:S(2)}) copy-start(bf16[1,192,2048]{2,1,0:T(8,128)(2,1)} %param.21) | copy-start | bytes 2359300
  128.4 29.0 %collective-permute-start.8 = (bf16[288,2048]{1,0:T(8,128)(2,1)S(1)}, bf16[288,2048]{1,0:T(8,128)(2,1)S(1)}, u32[]{:S(2)}, u32[]{:S(2)}) collective-permute-start(bf16[288,2048]{1,0:T(8,128)(2,1)S(1)} %slice.56), channel_id=1, source_target_pairs={{0,128},{128,256},{256,384},{384,0},{1,129},{129,257},{257,385},{3... | collective-permute-start | bytes 3538952 | tf_op jit(solution)/shard_map/ppermute | solution.py:17
  133.0 28.8 %collective-permute-start.9 = (bf16[288,2048]{1,0:T(8,128)(2,1)S(1)}, bf16[288,2048]{1,0:T(8,128)(2,1)S(1)}, u32[]{:S(2)}, u32[]{:S(2)}) collective-permute-start(bf16[288,2048]{1,0:T(8,128)(2,1)S(1)} %slice.57), channel_id=1, source_target_pairs={{0,384},{128,0},{256,128},{384,256},{1,385},{129,1},{257,129},{385... | collective-permute-start | bytes 3538952 | tf_op jit(solution)/shard_map/ppermute | solution.py:17
  168.1 1.0 copy-start.2
  169.1 21.2 %copy-start.15 = (bf16[8,2,2,4,128]{4,3,2,1,0:T(4,128)(2,1)S(1)}, bf16[8,2,2,4,128]{4,3,2,1,0:T(4,128)(2,1)}, u32[]{:S(2)}) copy-start(bf16[8,2,2,4,128]{4,3,2,1,0:T(4,128)(2,1)} %param.15) | copy-start | bytes 98308
  169.1 22.5 %copy-start.9 = (bf16[256,2,4,128]{3,2,1,0:T(4,128)(2,1)S(1)}, bf16[256,2,4,128]{3,2,1,0:T(4,128)(2,1)}, u32[]{:S(2)}) copy-start(bf16[256,2,4,128]{3,2,1,0:T(4,128)(2,1)} %param.12) | copy-start | bytes 1572868
  171.7 20.8 %copy-start.6 = (bf16[128,2,1024]{2,1,0:T(2,128)(2,1)}, bf16[128,2,1024]{2,1,0:T(2,128)(2,1)S(1)}, u32[]{:S(2)}) copy-start(bf16[128,2,1024]{2,1,0:T(2,128)(2,1)S(1)} %all-to-all-done.1) | copy-start | bytes 1572868
  171.7 72.9 %all-to-all-start.3 = ((bf16[128,2,2048]{2,1,0:T(2,128)(2,1)}), bf16[128,2,2048]{2,1,0:T(2,128)(2,1)S(1)}, u32[]{:S(2)}, u32[]{:S(2)}) async-start(bf16[128,2,2048]{2,1,0:T(2,128)(2,1)} %reshape.136), calls=%async_computation.3 | async-start | bytes 2097152 | tf_op jit(solution)/shard_map/all_to_all | solution.py:286
  194.7 2.5 %copy-start.7 = (bf16[8,32,2,4,128]{4,3,2,1,0:T(4,128)(2,1)}, bf16[8,32,2,4,128]{4,3,2,1,0:T(4,128)(2,1)S(1)}, u32[]{:S(2)}) copy-start(bf16[8,32,2,4,128]{4,3,2,1,0:T(4,128)(2,1)S(1)} %reshape.128) | copy-start | bytes 1572868
  194.7 1.8 copy-start.14
  197.2 0.7 copy-start.16

commit v2 on v1

--- a/solution.py
+++ b/solution.py
@@ -32,9 +32,15 @@
     return [wide] + [shift(wide, "ep_0", 16, step) for step in (1, -1, 2)]
 
 
-def select_body(place_ref, own_ref, back_ref, ahead_ref, far_ref, out_ref, rows_ref, *, width):
-    for n, part in enumerate((own_ref, back_ref, ahead_ref, far_ref)):
-        rows_ref[n * 64 : (n + 1) * 64, :] = part[...]
+def select_body(place_ref, own_ref, back_ref, ahead_ref, far_ref, out_ref, rows_ref, sems, *, width):
+    copies = [
+        pltpu.make_async_copy(part, rows_ref.at[n * 64 : (n + 1) * 64], sems.at[n])
+        for n, part in enumerate((own_ref, back_ref, ahead_ref, far_ref))
+    ]
+    for copy in copies:
+        copy.start()
+    for copy in copies:
+        copy.wait()
     count = rows_ref.shape[0]
     slots = out_ref.shape[0]
     place = place_ref[0]
@@ -68,19 +74,22 @@
 
 def select_rows(place, blocks, width, slots):
     rows = sum(b.shape[0] for b in blocks)
-    spec = pl.BlockSpec(memory_space=pltpu.VMEM)
     return pl.pallas_call(
         lambda *refs: select_body(*refs, width=width),
         out_shape=jax.ShapeDtypeStruct((slots, width), jnp.bfloat16),
-        in_specs=[pl.BlockSpec(memory_space=pltpu.SMEM)] + [spec] * 4,
-        out_specs=spec,
-        scratch_shapes=[pltpu.VMEM((rows, blocks[0].shape[1]), jnp.bfloat16)],
+        in_specs=[pl.BlockSpec(memory_space=pltpu.SMEM)]
+        + [pl.BlockSpec(memory_space=pl.ANY)] * 4,
+        out_specs=pl.BlockSpec(memory_space=pltpu.VMEM),
+        scratch_shapes=[
+            pltpu.VMEM((rows, blocks[0].shape[1]), jnp.bfloat16),
+            pltpu.SemaphoreType.DMA((4,)),
+        ],
         name="select_rows",
     )(place.reshape(1), *blocks)
 
 
 def expert_body(
-    rows_hbm, in_hbm, out_hbm, before_hbm, after_hbm, low_hbm, high_hbm, result_hbm,
+    rows_hbm, own_hbm, before_hbm, after_hbm, low_hbm, high_hbm, result_hbm,
     rows, own, before, after, far, result, sems,
 ):
     hidden = own.shape[0] // 3
@@ -90,8 +99,7 @@
         for n, (src, dst) in enumerate(
             (
                 (rows_hbm, rows),
-                (in_hbm, own.at[: 2 * hidden]),
-                (out_hbm, own.at[2 * hidden :]),
+                (own_hbm, own),
                 (before_hbm, before),
                 (after_hbm, after),
                 (low_hbm, far.at[:half]),
@@ -108,7 +116,7 @@
     order = order.astype(jnp.float32).astype(jnp.bfloat16)
     total = None
     contract = (((1,), (1,)), ((), ()))
-    for weights, waits in ((own, (0, 1, 2)), (before, (3,)), (after, (4,)), (far, (5, 6))):
+    for weights, waits in ((own, (0, 1)), (before, (2,)), (after, (3,)), (far, (4, 5))):
         for n in waits:
             copies[n].wait()
         both = lax.dot_general(
@@ -119,26 +127,25 @@
         act = jnp.dot(order, act, preferred_element_type=jnp.float32).astype(jnp.bfloat16)
         part = jnp.dot(act, weights[2 * hidden :], preferred_element_type=jnp.float32)
         total = part if total is None else total + part
-    result[...] = total.astype(jnp.bfloat16)
-    last = pltpu.make_async_copy(result, result_hbm, sems.at[7])
+    result[...] = total.astype(jnp.bfloat16).reshape(result.shape)
+    last = pltpu.make_async_copy(result, result_hbm, sems.at[6])
     last.start()
     last.wait()
 
 
-def expert(rows, in_own, out_own, before, after, low, high):
+def expert(rows, own, before, after, low, high):
     count, width = rows.shape
-    span = before.shape[0]
     return pl.pallas_call(
         expert_body,
-        out_shape=jax.ShapeDtypeStruct((count, width), jnp.bfloat16),
-        in_specs=[pl.BlockSpec(memory_space=pl.ANY)] * 7,
-        out_specs=pl.BlockSpec(memory_space=pl.ANY),
+        out_shape=jax.ShapeDtypeStruct((count // 2, 2, width), jnp.bfloat16),
+        in_specs=[pl.BlockSpec(memory_space=pl.ANY)] + [pl.BlockSpec(memory_space=pltpu.HBM)] * 5,
+        out_specs=pl.BlockSpec(memory_space=pltpu.HBM),
         scratch_shapes=[pltpu.VMEM((count, width), jnp.bfloat16)]
-        + [pltpu.VMEM((span, width), jnp.bfloat16)] * 4
-        + [pltpu.VMEM((count, width), jnp.bfloat16), pltpu.SemaphoreType.DMA((8,))],
+        + [pltpu.VMEM(own.shape, jnp.bfloat16)] * 4
+        + [pltpu.VMEM((count // 2, 2, width), jnp.bfloat16), pltpu.SemaphoreType.DMA((7,))],
         compiler_params=pltpu.CompilerParams(vmem_limit_bytes=32 * 1024 * 1024),
         name="expert",
-    )(rows, in_own, out_own, before, after, low, high)
+    )(rows, own, before, after, low, high)
 
 
 def attend(queries, gen_block, new_block, prompt_cache):
@@ -227,7 +234,8 @@
 
     in_own = w_gate_up.reshape(width, 2 * half_cols).T
     out_own = w_down.reshape(half_cols, width)
-    before, after, low, high = ring_gather(jnp.concatenate([in_own, out_own], axis=0))
+    own = jnp.concatenate([in_own, out_own], axis=0)
+    before, after, low, high = ring_gather(own)
 
     piece_len = gen_cache.size // (per_dev * ep_count)
     flat_cache = (
@@ -277,8 +285,7 @@
         concat_axis=0,
         tiled=True,
     ).reshape(slot_count, width)
-    produced = expert(rows, in_own, out_own, before, after, low, high)
-    produced = produced.reshape(ep_count, per_expert, width)
+    produced = expert(rows, own, before, after, low, high)
 
     slot_ids = slot_numbers(own_routes, per_expert)
     hits = jnp.arange(slot_count, dtype=jnp.int32)[:, None, None] == slot_ids[None, :, :]

time: 247 us -> 243 us (0.984)
  local copies, waits for them, and re-layouts: 27.3 us -> 23.9 us
    reshape x1 -> x0, local copies, waits for them, and re-layouts: 2.6 us -> none  [shards(): produced = produced.reshape(ep_count, per_expert, width)]
  transfers between devices with their start and end apart: 14 -> 14, of which waited for: 10 -> 10; matrix products, arithmetic and copies ran while one was open for 12% -> 11% of each run, Pallas kernels for 4% -> 4%
where the time goes in v2:
time: 243 us; the launch traced here: 242 us
  waiting for transfers between devices  109 us (45%)
  starting transfers between devices  88.1 us (36%)
  local copies, waits for them, and re-layouts  23.9 us (10%)
  Pallas kernels  10.1 us (4%)
  other arithmetic  6.2 us (3%)
  matrix products  3.72 us (2%)
    ppermute x10, waiting for transfers between devices, shift(): lax.ppermute(block, axis, [(i, (i + step) % count) for i in range(count)])  59.3 us
    all_to_all x1, waiting for transfers between devices, shards(): lax.all_to_all(produced, EP, split_axis=0, concat_axis=0, tiled=True)  44.8 us
    ppermute x10, starting transfers between devices, shift(): lax.ppermute(block, axis, [(i, (i + step) % count) for i in range(count)])  38.4 us
    all_to_all x1, starting transfers between devices, shards(): lax.all_to_all(flat_cache, EP, split_axis=0, concat_axis=0, tiled=True)  19.3 us
    all_to_all x1, starting transfers between devices, shards(): lax.all_to_all(produced, EP, split_axis=0, concat_axis=0, tiled=True)  17.4 us
    all_to_all x1, starting transfers between devices, shards(): moved = lax.all_to_all(chosen, EP, split_axis=0, concat_axis=0, tiled=True)  7.55 us
    pallas_call x1, Pallas kernels, expert(): pl.pallas_call(expert_body, out_shape=jax.ShapeDtypeStruct((count // 2, 2...  6.72 us
    all_to_all x1, starting transfers between devices, shards(): lax.all_to_all(packed.reshape(local, planes * per_expert, width), EP[1:],...  5.43 us
  transfers between devices with their start and end apart: 14, of which 10 were waited for; matrix products, arithmetic and copies ran while one was open for 11% of the time, Pallas kernels for 4%

profile of v2, /device:TPU:41, one launch (start us, length us, event | category | flops | bytes accessed | tf_op | source)
XLA Modules:
  0.0 241.8 jit_solution(6049894500833012909)
XLA Ops:
  1.4 1.4 reshape.120
  3.4 1.7 copy.154
  5.1 19.3 %all-to-all-start = ((bf16[128,2,1152]{2,1,0:T(2,128)(2,1)}), bf16[128,2,1152]{2,1,0:T(2,128)(2,1)S(1)}, u32[]{:S(2)}, u32[]{:S(2)}) async-start(bf16[128,2,1152]{2,1,0:T(2,128)(2,1)} %copy.154), calls=%async_computation | async-start | bytes 1179648 | tf_op jit(solution)/shard_map/all_to_all | solution.py:252
  25.5 7.2 %collective-permute-start = (bf16[16,2176]{1,0:T(8,128)(2,1)S(1)}, bf16[16,2176]{1,0:T(8,128)(2,1)S(1)}, u32[]{:S(2)}, u32[]{:S(2)}) collective-permute-start(bf16[16,2176]{1,0:T(8,128)(2,1)S(1)} %pad_maximum_fusion.3), channel_id=1, source_target_pairs={{0,32},{8,40},{16,48},{24,56},{32,64},{40,72},{48,80},{56,88},{64,... | collective-permute-start | bytes 208904 | tf_op jit(solution)/shard_map/ppermute | solution.py:17
  32.7 2.0 collective-permute-start.1
  34.7 11.3 %collective-permute-start.2 = (bf16[16,2176]{1,0:T(8,128)(2,1)S(1)}, bf16[16,2176]{1,0:T(8,128)(2,1)S(1)}, u32[]{:S(2)}, u32[]{:S(2)}) collective-permute-start(bf16[16,2176]{1,0:T(8,128)(2,1)S(1)} %pad_maximum_fusion.3), channel_id=1, source_target_pairs={{0,64},{8,72},{16,80},{24,88},{32,96},{40,104},{48,112},{56,120},{... | collective-permute-start | bytes 208904 | tf_op jit(solution)/shard_map/ppermute | solution.py:17
  46.0 1.8 pad_maximum_fusion.own_hbm
  47.8 3.2 %collective-permute-start.6 = (bf16[576,2048]{1,0:T(8,128)(2,1)S(1)}, bf16[576,2048]{1,0:T(8,128)(2,1)}, u32[]{:S(2)}, u32[]{:S(2)}) collective-permute-start(bf16[576,2048]{1,0:T(8,128)(2,1)S(1)} %pad_maximum_fusion.own_hbm), channel_id=1, source_target_pairs={{0,128},{128,256},{256,384},{384,0},{1,129},{129,257},{257,385},{3... | collective-permute-start | bytes 7077896 | tf_op jit(solution)/shard_map/ppermute | solution.py:17
  51.0 2.1 collective-permute-start.7
  53.1 4.7 %collective-permute-done = bf16[16,2176]{1,0:T(8,128)(2,1)S(1)} collective-permute-done((bf16[16,2176]{1,0:T(8,128)(2,1)S(1)}, bf16[16,2176]{1,0:T(8,128)(2,1)S(1)}, u32[]{:S(2)}, u32[]{:S(2)}) %collective-permute-start) | collective-permute-done | bytes 69664 | tf_op jit(solution)/shard_map/ppermute | solution.py:17
  57.8 2.2 collective-permute-done.1
  60.0 9.5 %collective-permute-done.2 = bf16[16,2176]{1,0:T(8,128)(2,1)S(1)} collective-permute-done((bf16[16,2176]{1,0:T(8,128)(2,1)S(1)}, bf16[16,2176]{1,0:T(8,128)(2,1)S(1)}, u32[]{:S(2)}, u32[]{:S(2)}) %collective-permute-start.2) | collective-permute-done | bytes 69664 | tf_op jit(solution)/shard_map/ppermute | solution.py:17
  69.6 1.9 collective-permute-start.3
  71.5 3.4 %collective-permute-start.4 = (bf16[64,2176]{1,0:T(8,128)(2,1)S(1)}, bf16[64,2176]{1,0:T(8,128)(2,1)}, u32[]{:S(2)}, u32[]{:S(2)}) collective-permute-start(bf16[64,2176]{1,0:T(8,128)(2,1)S(1)} %pad_maximum_fusion.2.refs_1_), channel_id=1, source_target_pairs={{0,120},{8,0},{16,8},{24,16},{32,24},{40,32},{48,40},{56,48},{64,5... | collective-permute-start | bytes 835592 | tf_op jit(solution)/shard_map/ppermute | solution.py:17
  74.9 1.9 collective-permute-start.5
  78.1 2.2 collective-permute-done.4.refs_3_
  80.3 12.9 %collective-permute-done.5.refs_4_ = bf16[64,2176]{1,0:T(8,128)(2,1)} collective-permute-done((bf16[64,2176]{1,0:T(8,128)(2,1)S(1)}, bf16[64,2176]{1,0:T(8,128)(2,1)}, u32[]{:S(2)}, u32[]{:S(2)}) %collective-permute-start.5) | collective-permute-done | bytes 278560 | tf_op jit(solution)/shard_map/ppermute | solution.py:17
  93.2 3.4 %select_rows.1 = bf16[256,2048]{1,0:T(8,128)(2,1)} custom-call(s32[1]{0:T(128)} %bitcast.33.refs_0_, bf16[64,2176]{1,0:T(8,128)(2,1)} %copy-done.4, bf16[64,2176]{1,0:T(8,128)(2,1)} %collective-permute-done.3.refs_2_, bf16[64,2176]{1,0:T(8,128)(2,1)} %collective-permute-done.4.refs_3_, bf16[64,2176]{1,0:T(8,128)(2,1)} %collective-permute-done.5.refs_4_), custom_call_target="tpu_custom_call" | custom-call | tf_op jit(solution)/shard_map/select_rows/pallas_call | solution.py:77
  96.7 5.4 %all-to-all-start.2 = ((bf16[8,32,2048]{2,1,0:T(8,128)(2,1)}), bf16[8,32,2048]{2,1,0:T(8,128)(2,1)}, u32[]{:S(2)}, u32[]{:S(2)}) async-start(bf16[8,32,2048]{2,1,0:T(8,128)(2,1)} %bitcast.87), calls=%async_computation.2 | async-start | bytes 2097152 | tf_op jit(solution)/shard_map/all_to_all | solution.py:281
  105.6 5.0 %gather_fusion = bf16[1024,256]{1,0:T(8,128)(2,1)} fusion(bf16[1024,256]{1,0:T(8,128)(2,1)S(1)} %reshape.122, s32[1024]{0:T(1024)S(1)} %broadcast_clamp_fusion), kind=kCustom, calls=%fused_computation | custom fusion | bytes 1052672 | tf_op jit(solution)/shard_map/jit(_take)/gather | solution.py:256
  110.6 2.0 reshape.123
  112.6 4.6 %all-to-all-done.2 = bf16[8,32,2048]{2,1,0:T(8,128)(2,1)} async-done(((bf16[8,32,2048]{2,1,0:T(8,128)(2,1)}), bf16[8,32,2048]{2,1,0:T(8,128)(2,1)}, u32[]{:S(2)}, u32[]{:S(2)}) %all-to-all-start.2) | async-done | bytes 1048608 | tf_op jit(solution)/shard_map/all_to_all | solution.py:281
  117.2 7.6 %all-to-all-start.1 = ((bf16[128,2,1024]{2,1,0:T(2,128)(2,1)}), bf16[128,2,1024]{2,1,0:T(2,128)(2,1)S(1)}, u32[]{:S(2)}, u32[]{:S(2)}) async-start(bf16[128,2,1024]{2,1,0:T(2,128)(2,1)} %reshape.123), calls=%async_computation.1 | async-start | bytes 1048576 | tf_op jit(solution)/shard_map/all_to_all | solution.py:257
  124.7 1.4 slice.56
  126.1 3.2 %collective-permute-start.8 = (bf16[288,2048]{1,0:T(8,128)(2,1)S(1)}, bf16[288,2048]{1,0:T(8,128)(2,1)S(1)}, u32[]{:S(2)}, u32[]{:S(2)}) collective-permute-start(bf16[288,2048]{1,0:T(8,128)(2,1)S(1)} %slice.56), channel_id=1, source_target_pairs={{0,128},{128,256},{256,384},{384,0},{1,129},{129,257},{257,385},{3... | collective-permute-start | bytes 3538952 | tf_op jit(solution)/shard_map/ppermute | solution.py:17
  129.3 1.4 slice.57
  130.7 2.3 collective-permute-start.9
  133.0 22.1 %collective-permute-done.8.low_hbm = bf16[288,2048]{1,0:T(8,128)(2,1)S(1)} collective-permute-done((bf16[288,2048]{1,0:T(8,128)(2,1)S(1)}, bf16[288,2048]{1,0:T(8,128)(2,1)S(1)}, u32[]{:S(2)}, u32[]{:S(2)}) %collective-permute-start.8) | collective-permute-done | bytes 1179680 | tf_op jit(solution)/shard_map/ppermute | solution.py:17
  155.1 4.3 %collective-permute-done.9.high_hbm = bf16[288,2048]{1,0:T(8,128)(2,1)S(1)} collective-permute-done((bf16[288,2048]{1,0:T(8,128)(2,1)S(1)}, bf16[288,2048]{1,0:T(8,128)(2,1)S(1)}, u32[]{:S(2)}, u32[]{:S(2)}) %collective-permute-start.9) | collective-permute-done | bytes 1179680 | tf_op jit(solution)/shard_map/ppermute | solution.py:17
  159.5 6.7 %expert.1 = bf16[128,2,2048]{2,1,0:T(2,128)(2,1)S(1)} custom-call(bf16[256,2048]{1,0:T(8,128)(2,1)} %bitcast.36.rows_hbm, bf16[576,2048]{1,0:T(8,128)(2,1)S(1)} %pad_maximum_fusion.own_hbm, bf16[576,2048]{1,0:T(8,128)(2,1)} %collective-permute-done.6.before_hbm, bf16[576,2048]{1,0:T(8,128)(2,1)} %collective-permute-done.7.after_hbm, ...), custom_call_target="tpu_custom_call" | custom-call | tf_op jit(solution)/shard_map/expert/pallas_call | solution.py:138
  167.2 17.4 %all-to-all-start.3 = ((bf16[128,2,2048]{2,1,0:T(2,128)(2,1)}), bf16[128,2,2048]{2,1,0:T(2,128)(2,1)S(1)}, u32[]{:S(2)}, u32[]{:S(2)}) async-start(bf16[128,2,2048]{2,1,0:T(2,128)(2,1)} %copy-done.1), calls=%async_computation.3 | async-start | bytes 2097152 | tf_op jit(solution)/shard_map/all_to_all | solution.py:293
  195.4 44.8 %all-to-all-done.3 = bf16[128,2,2048]{2,1,0:T(2,128)(2,1)S(1)} async-done(((bf16[128,2,2048]{2,1,0:T(2,128)(2,1)}), bf16[128,2,2048]{2,1,0:T(2,128)(2,1)S(1)}, u32[]{:S(2)}, u32[]{:S(2)}) %all-to-all-start.3) | async-done | bytes 1048608 | tf_op jit(solution)/shard_map/all_to_all | solution.py:293
  (80 shorter events, 20.3 us)
Async XLA Ops:
  0.6 185.9 %copy-start = (bf16[8,2,64,128]{3,2,1,0:T(8,128)(2,1)S(1)}, bf16[8,2,64,128]{3,2,1,0:T(8,128)(2,1)}, u32[]{:S(2)}) copy-start(bf16[8,2,64,128]{3,2,1,0:T(8,128)(2,1)} %param.14) | copy-start | bytes 786436
  2.7 21.7 %copy-start.6 = (bf16[8,2,2048]{2,1,0:T(2,128)(2,1)S(1)}, bf16[8,2,2048]{2,1,0:T(2,128)(2,1)}, u32[]{:S(2)}) copy-start(bf16[8,2,2048]{2,1,0:T(2,128)(2,1)} %param.16) | copy-start | bytes 196612
  2.7 22.7 %copy-start.10 = (f32[2048]{0:T(1024)S(1)}, f32[2048]{0:T(1024)}, u32[]{:S(2)}) copy-start(f32[2048]{0:T(1024)} %param.17) | copy-start | bytes 24580
  5.1 91.5 %all-to-all-start = ((bf16[128,2,1152]{2,1,0:T(2,128)(2,1)}), bf16[128,2,1152]{2,1,0:T(2,128)(2,1)S(1)}, u32[]{:S(2)}, u32[]{:S(2)}) async-start(bf16[128,2,1152]{2,1,0:T(2,128)(2,1)} %copy.154), calls=%async_computation | async-start | bytes 1179648 | tf_op jit(solution)/shard_map/all_to_all | solution.py:252
  25.5 32.3 %collective-permute-start = (bf16[16,2176]{1,0:T(8,128)(2,1)S(1)}, bf16[16,2176]{1,0:T(8,128)(2,1)S(1)}, u32[]{:S(2)}, u32[]{:S(2)}) collective-permute-start(bf16[16,2176]{1,0:T(8,128)(2,1)S(1)} %pad_maximum_fusion.3), channel_id=1, source_target_pairs={{0,32},{8,40},{16,48},{24,56},{32,64},{40,72},{48,80},{56,88},{64,... | collective-permute-start | bytes 208904 | tf_op jit(solution)/shard_map/ppermute | solution.py:17
  32.7 27.4 %collective-permute-start.1 = (bf16[16,2176]{1,0:T(8,128)(2,1)S(1)}, bf16[16,2176]{1,0:T(8,128)(2,1)S(1)}, u32[]{:S(2)}, u32[]{:S(2)}) collective-permute-start(bf16[16,2176]{1,0:T(8,128)(2,1)S(1)} %pad_maximum_fusion.3), channel_id=1, source_target_pairs={{0,96},{8,104},{16,112},{24,120},{32,0},{40,8},{48,16},{56,24},{64... | collective-permute-start | bytes 208904 | tf_op jit(solution)/shard_map/ppermute | solution.py:17
  34.7 34.9 %collective-permute-start.2 = (bf16[16,2176]{1,0:T(8,128)(2,1)S(1)}, bf16[16,2176]{1,0:T(8,128)(2,1)S(1)}, u32[]{:S(2)}, u32[]{:S(2)}) collective-permute-start(bf16[16,2176]{1,0:T(8,128)(2,1)S(1)} %pad_maximum_fusion.3), channel_id=1, source_target_pairs={{0,64},{8,72},{16,80},{24,88},{32,96},{40,104},{48,112},{56,120},{... | collective-permute-start | bytes 208904 | tf_op jit(solution)/shard_map/ppermute | solution.py:17
  47.8 76.9 %collective-permute-start.6 = (bf16[576,2048]{1,0:T(8,128)(2,1)S(1)}, bf16[576,2048]{1,0:T(8,128)(2,1)}, u32[]{:S(2)}, u32[]{:S(2)}) collective-permute-start(bf16[576,2048]{1,0:T(8,128)(2,1)S(1)} %pad_maximum_fusion.own_hbm), channel_id=1, source_target_pairs={{0,128},{128,256},{256,384},{384,0},{1,129},{129,257},{257,385},{3... | collective-permute-start | bytes 7077896 | tf_op jit(solution)/shard_map/ppermute | solution.py:17
  51.0 78.3 %collective-permute-start.7 = (bf16[576,2048]{1,0:T(8,128)(2,1)S(1)}, bf16[576,2048]{1,0:T(8,128)(2,1)}, u32[]{:S(2)}, u32[]{:S(2)}) collective-permute-start(bf16[576,2048]{1,0:T(8,128)(2,1)S(1)} %pad_maximum_fusion.own_hbm), channel_id=1, source_target_pairs={{0,384},{128,0},{256,128},{384,256},{1,385},{129,1},{257,129},{385... | collective-permute-start | bytes 7077896 | tf_op jit(solution)/shard_map/ppermute | solution.py:17
  69.6 23.6 %copy-start.4 = (bf16[64,2176]{1,0:T(8,128)(2,1)}, bf16[64,2176]{1,0:T(8,128)(2,1)S(1)}, u32[]{:S(2)}) copy-start(bf16[64,2176]{1,0:T(8,128)(2,1)S(1)} %pad_maximum_fusion.2.refs_1_) | copy-start | bytes 835588
  69.6 8.5 %collective-permute-start.3 = (bf16[64,2176]{1,0:T(8,128)(2,1)S(1)}, bf16[64,2176]{1,0:T(8,128)(2,1)}, u32[]{:S(2)}, u32[]{:S(2)}) collective-permute-start(bf16[64,2176]{1,0:T(8,128)(2,1)S(1)} %pad_maximum_fusion.2.refs_1_), channel_id=1, source_target_pairs={{0,8},{8,16},{16,24},{24,32},{32,40},{40,48},{48,56},{56,64},{64,7... | collective-permute-start | bytes 835592 | tf_op jit(solution)/shard_map/ppermute | solution.py:17
  71.5 8.8 %collective-permute-start.4 = (bf16[64,2176]{1,0:T(8,128)(2,1)S(1)}, bf16[64,2176]{1,0:T(8,128)(2,1)}, u32[]{:S(2)}, u32[]{:S(2)}) collective-permute-start(bf16[64,2176]{1,0:T(8,128)(2,1)S(1)} %pad_maximum_fusion.2.refs_1_), channel_id=1, source_target_pairs={{0,120},{8,0},{16,8},{24,16},{32,24},{40,32},{48,40},{56,48},{64,5... | collective-permute-start | bytes 835592 | tf_op jit(solution)/shard_map/ppermute | solution.py:17
  74.9 18.3 %collective-permute-start.5 = (bf16[64,2176]{1,0:T(8,128)(2,1)S(1)}, bf16[64,2176]{1,0:T(8,128)(2,1)}, u32[]{:S(2)}, u32[]{:S(2)}) collective-permute-start(bf16[64,2176]{1,0:T(8,128)(2,1)S(1)} %pad_maximum_fusion.2.refs_1_), channel_id=1, source_target_pairs={{0,16},{8,24},{16,32},{24,40},{32,48},{40,56},{48,64},{56,72},{64,... | collective-permute-start | bytes 835592 | tf_op jit(solution)/shard_map/ppermute | solution.py:17
  96.6 5.4 %copy-start.2 = (bf16[128,2,1152]{2,1,0:T(2,128)(2,1)}, bf16[128,2,1152]{2,1,0:T(2,128)(2,1)S(1)}, u32[]{:S(2)}) copy-start(bf16[128,2,1152]{2,1,0:T(2,128)(2,1)S(1)} %all-to-all-done) | copy-start | bytes 1769476
  96.7 20.5 %all-to-all-start.2 = ((bf16[8,32,2048]{2,1,0:T(8,128)(2,1)}), bf16[8,32,2048]{2,1,0:T(8,128)(2,1)}, u32[]{:S(2)}, u32[]{:S(2)}) async-start(bf16[8,32,2048]{2,1,0:T(8,128)(2,1)} %bitcast.87), calls=%async_computation.2 | async-start | bytes 2097152 | tf_op jit(solution)/shard_map/all_to_all | solution.py:281
  117.2 50.0 %all-to-all-start.1 = ((bf16[128,2,1024]{2,1,0:T(2,128)(2,1)}), bf16[128,2,1024]{2,1,0:T(2,128)(2,1)S(1)}, u32[]{:S(2)}, u32[]{:S(2)}) async-start(bf16[128,2,1024]{2,1,0:T(2,128)(2,1)} %reshape.123), calls=%async_computation.1 | async-start | bytes 1048576 | tf_op jit(solution)/shard_map/all_to_all | solution.py:257
  126.1 29.0 %collective-permute-start.8 = (bf16[288,2048]{1,0:T(8,128)(2,1)S(1)}, bf16[288,2048]{1,0:T(8,128)(2,1)S(1)}, u32[]{:S(2)}, u32[]{:S(2)}) collective-permute-start(bf16[288,2048]{1,0:T(8,128)(2,1)S(1)} %slice.56), channel_id=1, source_target_pairs={{0,128},{128,256},{256,384},{384,0},{1,129},{129,257},{257,385},{3... | collective-permute-start | bytes 3538952 | tf_op jit(solution)/shard_map/ppermute | solution.py:17
  130.7 28.8 %collective-permute-start.9 = (bf16[288,2048]{1,0:T(8,128)(2,1)S(1)}, bf16[288,2048]{1,0:T(8,128)(2,1)S(1)}, u32[]{:S(2)}, u32[]{:S(2)}) collective-permute-start(bf16[288,2048]{1,0:T(8,128)(2,1)S(1)} %slice.57), channel_id=1, source_target_pairs={{0,384},{128,0},{256,128},{384,256},{1,385},{129,1},{257,129},{385... | collective-permute-start | bytes 3538952 | tf_op jit(solution)/shard_map/ppermute | solution.py:17
  159.5 26.4 %copy-start.8 = (bf16[8,2,2,4,128]{4,3,2,1,0:T(4,128)(2,1)S(1)}, bf16[8,2,2,4,128]{4,3,2,1,0:T(4,128)(2,1)}, u32[]{:S(2)}) copy-start(bf16[8,2,2,4,128]{4,3,2,1,0:T(4,128)(2,1)} %param.15) | copy-start | bytes 98308
  166.2 1.0 copy-start.1
  167.2 20.1 %copy-start.5 = (bf16[256,2,4,128]{3,2,1,0:T(4,128)(2,1)S(1)}, bf16[256,2,4,128]{3,2,1,0:T(4,128)(2,1)}, u32[]{:S(2)}) copy-start(bf16[256,2,4,128]{3,2,1,0:T(4,128)(2,1)} %param.12) | copy-start | bytes 1572868
  167.2 73.0 %all-to-all-start.3 = ((bf16[128,2,2048]{2,1,0:T(2,128)(2,1)}), bf16[128,2,2048]{2,1,0:T(2,128)(2,1)S(1)}, u32[]{:S(2)}, u32[]{:S(2)}) async-start(bf16[128,2,2048]{2,1,0:T(2,128)(2,1)} %copy-done.1), calls=%async_computation.3 | async-start | bytes 2097152 | tf_op jit(solution)/shard_map/all_to_all | solution.py:293
  191.1 2.5 %copy-start.3 = (bf16[8,32,2,4,128]{4,3,2,1,0:T(4,128)(2,1)}, bf16[8,32,2,4,128]{4,3,2,1,0:T(4,128)(2,1)S(1)}, u32[]{:S(2)}) copy-start(bf16[8,32,2,4,128]{4,3,2,1,0:T(4,128)(2,1)S(1)} %reshape.125) | copy-start | bytes 1572868
  191.1 1.8 copy-start.7
  193.7 0.7 copy-start.9

commit v3 on v2

--- a/solution.py
+++ b/solution.py
@@ -9,8 +9,9 @@
 from jax.sharding import PartitionSpec as P
 
 
-EP = ("ep_0", "ep_1", "ep_2")
-REP_EP = ("rep", "ep_0", "ep_1", "ep_2")
+EP = ("wide", "near", "ep_1", "ep_2")
+REP_EP = ("rep",) + EP
+PLANES = EP[:2]
 
 
 def shift(block, axis, count, step):
@@ -27,9 +28,8 @@
 
 
 def ring_rows(block):
-    wide = [block] + [shift(block, "ep_0", 16, step) for step in (4, -4, 8)]
-    wide = jnp.concatenate(wide, axis=0)
-    return [wide] + [shift(wide, "ep_0", 16, step) for step in (1, -1, 2)]
+    wide = lax.all_gather(block, "wide", axis=0, tiled=True)
+    return [wide] + [shift(wide, PLANES, 16, step) for step in (1, -1, 2)]
 
 
 def select_body(place_ref, own_ref, back_ref, ahead_ref, far_ref, out_ref, rows_ref, sems, *, width):
@@ -47,8 +47,7 @@
     row = lax.broadcasted_iota(jnp.int32, (count, 1), 0)
     near, wide = row // 64, row // 16 % 4
     distance = jnp.where(near == 1, -1, jnp.where(near == 2, 1, jnp.where(near == 3, -2, 0)))
-    distance += jnp.where(wide == 1, -4, jnp.where(wide == 2, 4, jnp.where(wide == 3, -8, 0)))
-    source = (place + distance + 16) % 16
+    source = wide * 4 + (place + distance + 16) % 4
     column = lax.broadcasted_iota(jnp.int32, (count, slots), 1)
     expert = place * 8 + column // 32
     ids = rows_ref[:, width:].astype(jnp.int32)
@@ -148,6 +147,38 @@
     )(rows, own, before, after, low, high)
 
 
+def resample_body(pieces_any, out_ref, pieces_ref, sem):
+    copy = pltpu.make_async_copy(pieces_any, pieces_ref, sem)
+    copy.start()
+    copy.wait()
+    devices, two, width = pieces_ref.shape
+    count, length = devices * two, out_ref.shape[2]
+    rows = pieces_ref[...].reshape(count, width)
+    digits = rows[:, length : length + 8].astype(jnp.float32).astype(jnp.int32)
+    parents = digits[:, :4] * 256 + digits[:, 4:]
+    piece = length // 4
+    stacked = jnp.concatenate([rows[:, m * piece : (m + 1) * piece] for m in range(4)], axis=0)
+    column = lax.broadcasted_iota(jnp.int32, (count, 4 * count), 1)
+    particle = column % count * 4 + column // count
+    chosen = []
+    for m in range(4):
+        onehot = (parents[:, m : m + 1] == particle).astype(jnp.float32).astype(jnp.bfloat16)
+        picked = jnp.dot(onehot, stacked, preferred_element_type=jnp.float32)
+        chosen.append(picked.astype(jnp.bfloat16))
+    out_ref[...] = jnp.concatenate(chosen, axis=1).reshape(out_ref.shape)
+
+
+def resample(pieces, length):
+    return pl.pallas_call(
+        resample_body,
+        out_shape=jax.ShapeDtypeStruct(pieces.shape[:2] + (length,), jnp.bfloat16),
+        in_specs=[pl.BlockSpec(memory_space=pl.ANY)],
+        out_specs=pl.BlockSpec(memory_space=pltpu.VMEM),
+        scratch_shapes=[pltpu.VMEM(pieces.shape, jnp.bfloat16), pltpu.SemaphoreType.DMA(())],
+        name="resample",
+    )(pieces)
+
+
 def attend(queries, gen_block, new_block, prompt_cache):
     count = queries.shape[0]
     heads = queries.shape[2]
@@ -244,16 +275,14 @@
         .reshape(ep_count, 2, per_dev * piece_len // 2)
     )
     flat_len = flat_cache.shape[2]
-    digits = jnp.concatenate([ancestors // 256, ancestors % 256]).astype(jnp.bfloat16)
-    side = jnp.pad(digits, (0, 128 - digits.shape[0]))
+    fours = ancestors.reshape(2, per_dev // 2)
+    digits = jnp.concatenate([fours // 256, fours % 256], axis=1).astype(jnp.bfloat16)
+    side = jnp.pad(digits, ((0, 0), (0, 128 - digits.shape[1])))
     flat_cache = jnp.concatenate(
-        [flat_cache, jnp.broadcast_to(side, (ep_count, 2, side.shape[0]))], axis=2
+        [flat_cache, jnp.broadcast_to(side, (ep_count,) + side.shape)], axis=2
     )
     pieces = lax.all_to_all(flat_cache, EP, split_axis=0, concat_axis=0, tiled=True)
-    tail = pieces[:, 0, flat_len : flat_len + 2 * per_dev].astype(jnp.int32)
-    parents = (tail[:, :per_dev] * 256 + tail[:, per_dev:]).reshape(-1)
-    pieces = pieces[:, :, :flat_len].reshape(-1, piece_len)
-    chosen = jnp.take(pieces, parents, axis=0, mode="clip").reshape(ep_count, 2, flat_len)
+    chosen = resample(pieces, flat_len)
     moved = lax.all_to_all(chosen, EP, split_axis=0, concat_axis=0, tiled=True)
     cache_out = (
         moved.reshape(ep_count, per_dev, piece_len).transpose(1, 0, 2).reshape(gen_cache.shape)
@@ -275,12 +304,12 @@
     )
     labels = jnp.pad(own_routes.astype(jnp.bfloat16), ((0, 0), (0, 128 - top_count)))
     blocks = ring_rows(jnp.concatenate([normed, labels], axis=1))
-    planes = lax.axis_size("ep_0")
+    planes = lax.axis_size(PLANES)
     local = ep_count // planes
-    packed = select_rows(lax.axis_index("ep_0"), blocks, width, slot_count)
+    packed = select_rows(lax.axis_index(PLANES), blocks, width, slot_count)
     rows = lax.all_to_all(
         packed.reshape(local, planes * per_expert, width),
-        EP[1:],
+        EP[2:],
         split_axis=0,
         concat_axis=0,
         tiled=True,
@@ -303,7 +332,7 @@
 
 
 def solution(mesh):
-    torus = Mesh(mesh.devices.reshape(mesh.shape["rep"], 16, 4, 2), ("rep", "ep_0", "ep_1", "ep_2"))
+    torus = Mesh(mesh.devices.reshape(mesh.shape["rep"], 4, 4, 4, 2), REP_EP)
     placed = (
         P(REP_EP, None, None, None, None),
         P(),

time: 243 us -> 243 us (level)
  the two profiles are of different devices: /device:TPU:41 before, /device:TPU:33 now
where the time goes in v3:
time: 243 us; the launch traced here: 242 us
  waiting for transfers between devices  95.3 us (39%)
  starting transfers between devices  74.7 us (31%)
  blocking collectives  34.6 us (14%)
  local copies, waits for them, and re-layouts  13.4 us (6%)
  Pallas kernels  13.4 us (6%)
  other arithmetic  5.64 us (2%)
  matrix products  3.72 us (2%)
    all_to_all x1, waiting for transfers between devices, shards(): lax.all_to_all(produced, EP, split_axis=0, concat_axis=0, tiled=True)  45.1 us
    ppermute x7, waiting for transfers between devices, shift(): lax.ppermute(block, axis, [(i, (i + step) % count) for i in range(count)])  38.4 us
    all_gather x1, blocking collectives, ring_rows(): wide = lax.all_gather(block, 'wide', axis=0, tiled=True)  34.6 us
    ppermute x7, starting transfers between devices, shift(): lax.ppermute(block, axis, [(i, (i + step) % count) for i in range(count)])  23.1 us
    all_to_all x1, starting transfers between devices, shards(): lax.all_to_all(flat_cache, EP, split_axis=0, concat_axis=0, tiled=True)  19.3 us
    all_to_all x1, starting transfers between devices, shards(): lax.all_to_all(produced, EP, split_axis=0, concat_axis=0, tiled=True)  17.4 us
    all_to_all x1, waiting for transfers between devices, shards(): lax.all_to_all(packed.reshape(local, planes * per_expert, width), EP[2:],...  11.8 us
    all_to_all x1, starting transfers between devices, shards(): moved = lax.all_to_all(chosen, EP, split_axis=0, concat_axis=0, tiled=True)  9.27 us
  transfers between devices with their start and end apart: 11, of which 6 were waited for; matrix products, arithmetic and copies ran while one was open for 7% of the time, Pallas kernels for 6%

profile of v3, /device:TPU:33, one launch (start us, length us, event | category | flops | bytes accessed | tf_op | source)
XLA Modules:
  0.0 241.9 jit_solution(7626720001585756022)
XLA Ops:
  0.6 0.8 reshape.115
  1.4 1.4 reshape.113
  3.4 1.4 pad_maximum_fusion.1
  4.8 19.3 %all-to-all-start = ((bf16[128,2,1152]{2,1,0:T(2,128)(2,1)}), bf16[128,2,1152]{2,1,0:T(2,128)(2,1)S(1)}, u32[]{:S(2)}, u32[]{:S(2)}) async-start(bf16[128,2,1152]{2,1,0:T(2,128)(2,1)} %pad_maximum_fusion.1), calls=%async_computation | async-start | bytes 1179648 | tf_op jit(solution)/shard_map/all_to_all | solution.py:284
  24.1 1.8 pad_maximum_fusion.own_hbm
  26.0 3.2 %collective-permute-start.3 = (bf16[576,2048]{1,0:T(8,128)(2,1)S(1)}, bf16[576,2048]{1,0:T(8,128)(2,1)}, u32[]{:S(2)}, u32[]{:S(2)}) collective-permute-start(bf16[576,2048]{1,0:T(8,128)(2,1)S(1)} %pad_maximum_fusion.own_hbm), channel_id=1, source_target_pairs={{0,128},{128,256},{256,384},{384,0},{1,129},{129,257},{257,385},{3... | collective-permute-start | bytes 7077896 | tf_op jit(solution)/shard_map/ppermute | solution.py:18
  29.2 3.4 %collective-permute-start.4 = (bf16[576,2048]{1,0:T(8,128)(2,1)S(1)}, bf16[576,2048]{1,0:T(8,128)(2,1)}, u32[]{:S(2)}, u32[]{:S(2)}) collective-permute-start(bf16[576,2048]{1,0:T(8,128)(2,1)S(1)} %pad_maximum_fusion.own_hbm), channel_id=1, source_target_pairs={{0,384},{128,0},{256,128},{384,256},{1,385},{129,1},{257,129},{385... | collective-permute-start | bytes 7077896 | tf_op jit(solution)/shard_map/ppermute | solution.py:18
  33.6 34.6 %all_gather.3.refs_1_ = bf16[64,2176]{1,0:T(8,128)(2,1)S(1)} all-gather(bf16[16,2176]{1,0:T(8,128)(2,1)S(1)} %fusion.14), channel_id=1, replica_groups=mesh['rep'=4,'wide'=4,'near'=4,'ep_1'=4,'ep_2'=2] {'wide'}, dimensions={0}, use_global_device_ids=true | all-gather | bytes 348160 | tf_op jit(solution)/shard_map/all_gather | solution.py:31
  68.3 3.5 %collective-permute-start = (bf16[64,2176]{1,0:T(8,128)(2,1)S(1)}, bf16[64,2176]{1,0:T(8,128)(2,1)}, u32[]{:S(2)}, u32[]{:S(2)}) collective-permute-start(bf16[64,2176]{1,0:T(8,128)(2,1)S(1)} %all_gather.3.refs_1_), channel_id=1, source_target_pairs={{0,8},{8,16},{16,24},{24,32},{32,40},{40,48},{48,56},{56,64},{64,7... | collective-permute-start | bytes 835592 | tf_op jit(solution)/shard_map/ppermute | solution.py:18
  71.8 1.9 collective-permute-start.1
  73.7 4.4 %collective-permute-start.2 = (bf16[64,2176]{1,0:T(8,128)(2,1)S(1)}, bf16[64,2176]{1,0:T(8,128)(2,1)}, u32[]{:S(2)}, u32[]{:S(2)}) collective-permute-start(bf16[64,2176]{1,0:T(8,128)(2,1)S(1)} %all_gather.3.refs_1_), channel_id=1, source_target_pairs={{0,16},{8,24},{16,32},{24,40},{32,48},{40,56},{48,64},{56,72},{64,... | collective-permute-start | bytes 835592 | tf_op jit(solution)/shard_map/ppermute | solution.py:18
  78.1 2.9 %collective-permute-done.1.refs_3_ = bf16[64,2176]{1,0:T(8,128)(2,1)} collective-permute-done((bf16[64,2176]{1,0:T(8,128)(2,1)S(1)}, bf16[64,2176]{1,0:T(8,128)(2,1)}, u32[]{:S(2)}, u32[]{:S(2)}) %collective-permute-start.1) | collective-permute-done | bytes 278560 | tf_op jit(solution)/shard_map/ppermute | solution.py:18
  81.0 10.3 %collective-permute-done.2.refs_4_ = bf16[64,2176]{1,0:T(8,128)(2,1)} collective-permute-done((bf16[64,2176]{1,0:T(8,128)(2,1)S(1)}, bf16[64,2176]{1,0:T(8,128)(2,1)}, u32[]{:S(2)}, u32[]{:S(2)}) %collective-permute-start.2) | collective-permute-done | bytes 278560 | tf_op jit(solution)/shard_map/ppermute | solution.py:18
  91.3 3.4 %select_rows.1 = bf16[256,2048]{1,0:T(8,128)(2,1)} custom-call(s32[1]{0:T(128)} %bitcast.30.refs_0_, bf16[64,2176]{1,0:T(8,128)(2,1)} %copy-done.4, bf16[64,2176]{1,0:T(8,128)(2,1)} %collective-permute-done.refs_2_, bf16[64,2176]{1,0:T(8,128)(2,1)} %collective-permute-done.1.refs_3_, bf16[64,2176]{1,0:T(8,128)(2,1)} %collective-permute-done.2.refs_4_), custom_call_target="tpu_custom_call" | custom-call | tf_op jit(solution)/shard_map/select_rows/pallas_call | solution.py:76
  94.8 5.7 %all-to-all-start.2 = ((bf16[8,32,2048]{2,1,0:T(8,128)(2,1)}), bf16[8,32,2048]{2,1,0:T(8,128)(2,1)}, u32[]{:S(2)}, u32[]{:S(2)}) async-start(bf16[8,32,2048]{2,1,0:T(8,128)(2,1)} %bitcast.87), calls=%async_computation.2 | async-start | bytes 2097152 | tf_op jit(solution)/shard_map/all_to_all | solution.py:310
  100.4 3.3 %resample.1 = bf16[128,2,1024]{2,1,0:T(2,128)(2,1)} custom-call(bf16[128,2,1152]{2,1,0:T(2,128)(2,1)} %copy-done.2), custom_call_target="tpu_custom_call" | custom-call | tf_op jit(solution)/shard_map/resample/pallas_call | solution.py:172
  103.7 11.8 %all-to-all-done.2 = bf16[8,32,2048]{2,1,0:T(8,128)(2,1)} async-done(((bf16[8,32,2048]{2,1,0:T(8,128)(2,1)}), bf16[8,32,2048]{2,1,0:T(8,128)(2,1)}, u32[]{:S(2)}, u32[]{:S(2)}) %all-to-all-start.2) | async-done | bytes 1048608 | tf_op jit(solution)/shard_map/all_to_all | solution.py:310
  115.5 9.3 %all-to-all-start.1 = ((bf16[128,2,1024]{2,1,0:T(2,128)(2,1)}), bf16[128,2,1024]{2,1,0:T(2,128)(2,1)S(1)}, u32[]{:S(2)}, u32[]{:S(2)}) async-start(bf16[128,2,1024]{2,1,0:T(2,128)(2,1)} %resample.1), calls=%async_computation.1 | async-start | bytes 1048576 | tf_op jit(solution)/shard_map/all_to_all | solution.py:286
  124.8 1.4 slice.34
  126.2 3.2 %collective-permute-start.5 = (bf16[288,2048]{1,0:T(8,128)(2,1)S(1)}, bf16[288,2048]{1,0:T(8,128)(2,1)S(1)}, u32[]{:S(2)}, u32[]{:S(2)}) collective-permute-start(bf16[288,2048]{1,0:T(8,128)(2,1)S(1)} %slice.34), channel_id=1, source_target_pairs={{0,128},{128,256},{256,384},{384,0},{1,129},{129,257},{257,385},{3... | collective-permute-start | bytes 3538952 | tf_op jit(solution)/shard_map/ppermute | solution.py:18
  129.4 1.4 slice.35
  130.8 3.5 %collective-permute-start.6 = (bf16[288,2048]{1,0:T(8,128)(2,1)S(1)}, bf16[288,2048]{1,0:T(8,128)(2,1)S(1)}, u32[]{:S(2)}, u32[]{:S(2)}) collective-permute-start(bf16[288,2048]{1,0:T(8,128)(2,1)S(1)} %slice.35), channel_id=1, source_target_pairs={{0,384},{128,0},{256,128},{384,256},{1,385},{129,1},{257,129},{385... | collective-permute-start | bytes 3538952 | tf_op jit(solution)/shard_map/ppermute | solution.py:18
  134.4 22.2 %collective-permute-done.5.low_hbm = bf16[288,2048]{1,0:T(8,128)(2,1)S(1)} collective-permute-done((bf16[288,2048]{1,0:T(8,128)(2,1)S(1)}, bf16[288,2048]{1,0:T(8,128)(2,1)S(1)}, u32[]{:S(2)}, u32[]{:S(2)}) %collective-permute-start.5) | collective-permute-done | bytes 1179680 | tf_op jit(solution)/shard_map/ppermute | solution.py:18
  156.6 3.0 %collective-permute-done.6.high_hbm = bf16[288,2048]{1,0:T(8,128)(2,1)S(1)} collective-permute-done((bf16[288,2048]{1,0:T(8,128)(2,1)S(1)}, bf16[288,2048]{1,0:T(8,128)(2,1)S(1)}, u32[]{:S(2)}, u32[]{:S(2)}) %collective-permute-start.6) | collective-permute-done | bytes 1179680 | tf_op jit(solution)/shard_map/ppermute | solution.py:18
  159.6 6.7 %expert.1 = bf16[128,2,2048]{2,1,0:T(2,128)(2,1)S(1)} custom-call(bf16[256,2048]{1,0:T(8,128)(2,1)} %bitcast.33.rows_hbm, bf16[576,2048]{1,0:T(8,128)(2,1)S(1)} %pad_maximum_fusion.own_hbm, bf16[576,2048]{1,0:T(8,128)(2,1)} %collective-permute-done.3.before_hbm, bf16[576,2048]{1,0:T(8,128)(2,1)} %collective-permute-done.4.after_hbm, ...), custom_call_target="tpu_custom_call" | custom-call | tf_op jit(solution)/shard_map/expert/pallas_call | solution.py:137
  166.3 1.0 copy-done.1
  167.3 17.4 %all-to-all-start.3 = ((bf16[128,2,2048]{2,1,0:T(2,128)(2,1)}), bf16[128,2,2048]{2,1,0:T(2,128)(2,1)S(1)}, u32[]{:S(2)}, u32[]{:S(2)}) async-start(bf16[128,2,2048]{2,1,0:T(2,128)(2,1)} %copy-done.1), calls=%async_computation.3 | async-start | bytes 2097152 | tf_op jit(solution)/shard_map/all_to_all | solution.py:322
  186.5 0.8 fusion.27
  187.3 0.9 fusion.25
  188.6 1.0 reshape.116
  189.6 1.1 copy.191
  195.1 45.1 %all-to-all-done.3 = bf16[128,2,2048]{2,1,0:T(2,128)(2,1)S(1)} async-done(((bf16[128,2,2048]{2,1,0:T(2,128)(2,1)}), bf16[128,2,2048]{2,1,0:T(2,128)(2,1)S(1)}, u32[]{:S(2)}, u32[]{:S(2)}) %all-to-all-start.3) | async-done | bytes 1048608 | tf_op jit(solution)/shard_map/all_to_all | solution.py:322
  (67 shorter events, 9.9 us)
Async XLA Ops:
  0.6 185.9 %copy-start = (bf16[8,2,64,128]{3,2,1,0:T(8,128)(2,1)S(1)}, bf16[8,2,64,128]{3,2,1,0:T(8,128)(2,1)}, u32[]{:S(2)}) copy-start(bf16[8,2,64,128]{3,2,1,0:T(8,128)(2,1)} %param.14) | copy-start | bytes 786436
  4.8 89.9 %all-to-all-start = ((bf16[128,2,1152]{2,1,0:T(2,128)(2,1)}), bf16[128,2,1152]{2,1,0:T(2,128)(2,1)S(1)}, u32[]{:S(2)}, u32[]{:S(2)}) async-start(bf16[128,2,1152]{2,1,0:T(2,128)(2,1)} %pad_maximum_fusion.1), calls=%async_computation | async-start | bytes 1179648 | tf_op jit(solution)/shard_map/all_to_all | solution.py:284
  24.1 8.5 %copy-start.6 = (bf16[8,2,2048]{2,1,0:T(2,128)(2,1)S(1)}, bf16[8,2,2048]{2,1,0:T(2,128)(2,1)}, u32[]{:S(2)}) copy-start(bf16[8,2,2048]{2,1,0:T(2,128)(2,1)} %param.16) | copy-start | bytes 196612
  24.1 9.4 %copy-start.10 = (f32[2048]{0:T(1024)S(1)}, f32[2048]{0:T(1024)}, u32[]{:S(2)}) copy-start(f32[2048]{0:T(1024)} %param.17) | copy-start | bytes 24580
  26.0 98.9 %collective-permute-start.3 = (bf16[576,2048]{1,0:T(8,128)(2,1)S(1)}, bf16[576,2048]{1,0:T(8,128)(2,1)}, u32[]{:S(2)}, u32[]{:S(2)}) collective-permute-start(bf16[576,2048]{1,0:T(8,128)(2,1)S(1)} %pad_maximum_fusion.own_hbm), channel_id=1, source_target_pairs={{0,128},{128,256},{256,384},{384,0},{1,129},{129,257},{257,385},{3... | collective-permute-start | bytes 7077896 | tf_op jit(solution)/shard_map/ppermute | solution.py:18
  29.2 100.3 %collective-permute-start.4 = (bf16[576,2048]{1,0:T(8,128)(2,1)S(1)}, bf16[576,2048]{1,0:T(8,128)(2,1)}, u32[]{:S(2)}, u32[]{:S(2)}) collective-permute-start(bf16[576,2048]{1,0:T(8,128)(2,1)S(1)} %pad_maximum_fusion.own_hbm), channel_id=1, source_target_pairs={{0,384},{128,0},{256,128},{384,256},{1,385},{129,1},{257,129},{385... | collective-permute-start | bytes 7077896 | tf_op jit(solution)/shard_map/ppermute | solution.py:18
  68.3 23.0 %copy-start.4 = (bf16[64,2176]{1,0:T(8,128)(2,1)}, bf16[64,2176]{1,0:T(8,128)(2,1)S(1)}, u32[]{:S(2)}) copy-start(bf16[64,2176]{1,0:T(8,128)(2,1)S(1)} %all_gather.3.refs_1_) | copy-start | bytes 835588
  68.3 9.8 %collective-permute-start = (bf16[64,2176]{1,0:T(8,128)(2,1)S(1)}, bf16[64,2176]{1,0:T(8,128)(2,1)}, u32[]{:S(2)}, u32[]{:S(2)}) collective-permute-start(bf16[64,2176]{1,0:T(8,128)(2,1)S(1)} %all_gather.3.refs_1_), channel_id=1, source_target_pairs={{0,8},{8,16},{16,24},{24,32},{32,40},{40,48},{48,56},{56,64},{64,7... | collective-permute-start | bytes 835592 | tf_op jit(solution)/shard_map/ppermute | solution.py:18
  71.8 9.3 %collective-permute-start.1 = (bf16[64,2176]{1,0:T(8,128)(2,1)S(1)}, bf16[64,2176]{1,0:T(8,128)(2,1)}, u32[]{:S(2)}, u32[]{:S(2)}) collective-permute-start(bf16[64,2176]{1,0:T(8,128)(2,1)S(1)} %all_gather.3.refs_1_), channel_id=1, source_target_pairs={{0,120},{8,0},{16,8},{24,16},{32,24},{40,32},{48,40},{56,48},{64,5... | collective-permute-start | bytes 835592 | tf_op jit(solution)/shard_map/ppermute | solution.py:18
  73.7 17.6 %collective-permute-start.2 = (bf16[64,2176]{1,0:T(8,128)(2,1)S(1)}, bf16[64,2176]{1,0:T(8,128)(2,1)}, u32[]{:S(2)}, u32[]{:S(2)}) collective-permute-start(bf16[64,2176]{1,0:T(8,128)(2,1)S(1)} %all_gather.3.refs_1_), channel_id=1, source_target_pairs={{0,16},{8,24},{16,32},{24,40},{32,48},{40,56},{48,64},{56,72},{64,... | collective-permute-start | bytes 835592 | tf_op jit(solution)/shard_map/ppermute | solution.py:18
  94.7 5.7 %copy-start.2 = (bf16[128,2,1152]{2,1,0:T(2,128)(2,1)}, bf16[128,2,1152]{2,1,0:T(2,128)(2,1)S(1)}, u32[]{:S(2)}) copy-start(bf16[128,2,1152]{2,1,0:T(2,128)(2,1)S(1)} %all-to-all-done.pieces_any) | copy-start | bytes 1769476
  94.8 20.8 %all-to-all-start.2 = ((bf16[8,32,2048]{2,1,0:T(8,128)(2,1)}), bf16[8,32,2048]{2,1,0:T(8,128)(2,1)}, u32[]{:S(2)}, u32[]{:S(2)}) async-start(bf16[8,32,2048]{2,1,0:T(8,128)(2,1)} %bitcast.87), calls=%async_computation.2 | async-start | bytes 2097152 | tf_op jit(solution)/shard_map/all_to_all | solution.py:310
  115.5 51.7 %all-to-all-start.1 = ((bf16[128,2,1024]{2,1,0:T(2,128)(2,1)}), bf16[128,2,1024]{2,1,0:T(2,128)(2,1)S(1)}, u32[]{:S(2)}, u32[]{:S(2)}) async-start(bf16[128,2,1024]{2,1,0:T(2,128)(2,1)} %resample.1), calls=%async_computation.1 | async-start | bytes 1048576 | tf_op jit(solution)/shard_map/all_to_all | solution.py:286
  126.2 30.4 %collective-permute-start.5 = (bf16[288,2048]{1,0:T(8,128)(2,1)S(1)}, bf16[288,2048]{1,0:T(8,128)(2,1)S(1)}, u32[]{:S(2)}, u32[]{:S(2)}) collective-permute-start(bf16[288,2048]{1,0:T(8,128)(2,1)S(1)} %slice.34), channel_id=1, source_target_pairs={{0,128},{128,256},{256,384},{384,0},{1,129},{129,257},{257,385},{3... | collective-permute-start | bytes 3538952 | tf_op jit(solution)/shard_map/ppermute | solution.py:18
  130.8 28.7 %collective-permute-start.6 = (bf16[288,2048]{1,0:T(8,128)(2,1)S(1)}, bf16[288,2048]{1,0:T(8,128)(2,1)S(1)}, u32[]{:S(2)}, u32[]{:S(2)}) collective-permute-start(bf16[288,2048]{1,0:T(8,128)(2,1)S(1)} %slice.35), channel_id=1, source_target_pairs={{0,384},{128,0},{256,128},{384,256},{1,385},{129,1},{257,129},{385... | collective-permute-start | bytes 3538952 | tf_op jit(solution)/shard_map/ppermute | solution.py:18
  159.6 26.3 %copy-start.8 = (bf16[8,2,2,4,128]{4,3,2,1,0:T(4,128)(2,1)S(1)}, bf16[8,2,2,4,128]{4,3,2,1,0:T(4,128)(2,1)}, u32[]{:S(2)}) copy-start(bf16[8,2,2,4,128]{4,3,2,1,0:T(4,128)(2,1)} %param.15) | copy-start | bytes 98308
  166.3 1.0 copy-start.1
  167.3 20.0 %copy-start.5 = (bf16[256,2,4,128]{3,2,1,0:T(4,128)(2,1)S(1)}, bf16[256,2,4,128]{3,2,1,0:T(4,128)(2,1)}, u32[]{:S(2)}) copy-start(bf16[256,2,4,128]{3,2,1,0:T(4,128)(2,1)} %param.12) | copy-start | bytes 1572868
  167.3 73.0 %all-to-all-start.3 = ((bf16[128,2,2048]{2,1,0:T(2,128)(2,1)}), bf16[128,2,2048]{2,1,0:T(2,128)(2,1)S(1)}, u32[]{:S(2)}, u32[]{:S(2)}) async-start(bf16[128,2,2048]{2,1,0:T(2,128)(2,1)} %copy-done.1), calls=%async_computation.3 | async-start | bytes 2097152 | tf_op jit(solution)/shard_map/all_to_all | solution.py:322
  190.9 2.5 %copy-start.3 = (bf16[8,32,2,4,128]{4,3,2,1,0:T(4,128)(2,1)}, bf16[8,32,2,4,128]{4,3,2,1,0:T(4,128)(2,1)S(1)}, u32[]{:S(2)}) copy-start(bf16[8,32,2,4,128]{4,3,2,1,0:T(4,128)(2,1)S(1)} %reshape.117) | copy-start | bytes 1572868
  190.9 1.8 copy-start.7
  193.4 0.7 copy-start.9

commit v4 on v3

--- a/solution.py
+++ b/solution.py
@@ -28,7 +28,8 @@
 
 
 def ring_rows(block):
-    wide = lax.all_gather(block, "wide", axis=0, tiled=True)
+    wide = [block] + [shift(block, PLANES, 16, step) for step in (4, -4, 8)]
+    wide = jnp.concatenate(wide, axis=0)
     return [wide] + [shift(wide, PLANES, 16, step) for step in (1, -1, 2)]
 
 
@@ -47,7 +48,8 @@
     row = lax.broadcasted_iota(jnp.int32, (count, 1), 0)
     near, wide = row // 64, row // 16 % 4
     distance = jnp.where(near == 1, -1, jnp.where(near == 2, 1, jnp.where(near == 3, -2, 0)))
-    source = wide * 4 + (place + distance + 16) % 4
+    distance += jnp.where(wide == 1, -4, jnp.where(wide == 2, 4, jnp.where(wide == 3, -8, 0)))
+    source = (place + distance + 16) % 16
     column = lax.broadcasted_iota(jnp.int32, (count, slots), 1)
     expert = place * 8 + column // 32
     ids = rows_ref[:, width:].astype(jnp.int32)
@@ -88,8 +90,8 @@
 
 
 def expert_body(
-    rows_hbm, own_hbm, before_hbm, after_hbm, low_hbm, high_hbm, result_hbm,
-    rows, own, before, after, far, result, sems,
+    rows_hbm, own_hbm, before_hbm, after_hbm, low_hbm, high_hbm, result,
+    rows, own, before, after, far, sems,
 ):
     hidden = own.shape[0] // 3
     half = low_hbm.shape[0]
@@ -127,9 +129,6 @@
         part = jnp.dot(act, weights[2 * hidden :], preferred_element_type=jnp.float32)
         total = part if total is None else total + part
     result[...] = total.astype(jnp.bfloat16).reshape(result.shape)
-    last = pltpu.make_async_copy(result, result_hbm, sems.at[6])
-    last.start()
-    last.wait()
 
 
 def expert(rows, own, before, after, low, high):
@@ -138,10 +137,10 @@
         expert_body,
         out_shape=jax.ShapeDtypeStruct((count // 2, 2, width), jnp.bfloat16),
         in_specs=[pl.BlockSpec(memory_space=pl.ANY)] + [pl.BlockSpec(memory_space=pltpu.HBM)] * 5,
-        out_specs=pl.BlockSpec(memory_space=pltpu.HBM),
+        out_specs=pl.BlockSpec(memory_space=pltpu.VMEM),
         scratch_shapes=[pltpu.VMEM((count, width), jnp.bfloat16)]
         + [pltpu.VMEM(own.shape, jnp.bfloat16)] * 4
-        + [pltpu.VMEM((count // 2, 2, width), jnp.bfloat16), pltpu.SemaphoreType.DMA((7,))],
+        + [pltpu.SemaphoreType.DMA((6,))],
         compiler_params=pltpu.CompilerParams(vmem_limit_bytes=32 * 1024 * 1024),
         name="expert",
     )(rows, own, before, after, low, high)

time: 243 us -> 243 us (level)
  the two profiles are of different devices: /device:TPU:33 before, /device:TPU:41 now
where the time goes in v4:
time: 243 us; the launch traced here: 242 us
  waiting for transfers between devices  116 us (48%)
  starting transfers between devices  88.1 us (36%)
  local copies, waits for them, and re-layouts  13.4 us (6%)
  Pallas kernels  13.3 us (5%)
  other arithmetic  5.67 us (2%)
  matrix products  3.72 us (2%)
    ppermute x10, waiting for transfers between devices, shift(): lax.ppermute(block, axis, [(i, (i + step) % count) for i in range(count)])  59.3 us
    all_to_all x1, waiting for transfers between devices, shards(): lax.all_to_all(produced, EP, split_axis=0, concat_axis=0, tiled=True)  45.1 us
    ppermute x10, starting transfers between devices, shift(): lax.ppermute(block, axis, [(i, (i + step) % count) for i in range(count)])  38.4 us
    all_to_all x1, starting transfers between devices, shards(): lax.all_to_all(flat_cache, EP, split_axis=0, concat_axis=0, tiled=True)  19.3 us
    all_to_all x1, starting transfers between devices, shards(): lax.all_to_all(produced, EP, split_axis=0, concat_axis=0, tiled=True)  17.4 us
    all_to_all x1, waiting for transfers between devices, shards(): lax.all_to_all(packed.reshape(local, planes * per_expert, width), EP[2:],...  11.8 us
    all_to_all x1, starting transfers between devices, shards(): moved = lax.all_to_all(chosen, EP, split_axis=0, concat_axis=0, tiled=True)  7.56 us
    pallas_call x1, Pallas kernels, expert(): pl.pallas_call(expert_body, out_shape=jax.ShapeDtypeStruct((count // 2, 2...  6.62 us
  transfers between devices with their start and end apart: 14, of which 10 were waited for; matrix products, arithmetic and copies ran while one was open for 7% of the time, Pallas kernels for 6%

profile of v4, /device:TPU:41, one launch (start us, length us, event | category | flops | bytes accessed | tf_op | source)
XLA Modules:
  0.0 241.5 jit_solution(873111845970708735)
XLA Ops:
  1.4 1.4 reshape.113
  3.5 1.4 pad_maximum_fusion.1
  4.8 19.3 %all-to-all-start = ((bf16[128,2,1152]{2,1,0:T(2,128)(2,1)}), bf16[128,2,1152]{2,1,0:T(2,128)(2,1)S(1)}, u32[]{:S(2)}, u32[]{:S(2)}) async-start(bf16[128,2,1152]{2,1,0:T(2,128)(2,1)} %pad_maximum_fusion.1), calls=%async_computation | async-start | bytes 1179648 | tf_op jit(solution)/shard_map/all_to_all | solution.py:283
  25.3 7.2 %collective-permute-start = (bf16[16,2176]{1,0:T(8,128)(2,1)S(1)}, bf16[16,2176]{1,0:T(8,128)(2,1)S(1)}, u32[]{:S(2)}, u32[]{:S(2)}) collective-permute-start(bf16[16,2176]{1,0:T(8,128)(2,1)S(1)} %pad_maximum_fusion.3), channel_id=1, source_target_pairs={{0,32},{8,40},{16,48},{24,56},{32,64},{40,72},{48,80},{56,88},{64,... | collective-permute-start | bytes 208904 | tf_op jit(solution)/shard_map/ppermute | solution.py:18
  32.4 2.0 collective-permute-start.1
  34.5 11.3 %collective-permute-start.2 = (bf16[16,2176]{1,0:T(8,128)(2,1)S(1)}, bf16[16,2176]{1,0:T(8,128)(2,1)S(1)}, u32[]{:S(2)}, u32[]{:S(2)}) collective-permute-start(bf16[16,2176]{1,0:T(8,128)(2,1)S(1)} %pad_maximum_fusion.3), channel_id=1, source_target_pairs={{0,64},{8,72},{16,80},{24,88},{32,96},{40,104},{48,112},{56,120},{... | collective-permute-start | bytes 208904 | tf_op jit(solution)/shard_map/ppermute | solution.py:18
  45.8 1.8 pad_maximum_fusion.own_hbm
  47.6 3.2 %collective-permute-start.6 = (bf16[576,2048]{1,0:T(8,128)(2,1)S(1)}, bf16[576,2048]{1,0:T(8,128)(2,1)}, u32[]{:S(2)}, u32[]{:S(2)}) collective-permute-start(bf16[576,2048]{1,0:T(8,128)(2,1)S(1)} %pad_maximum_fusion.own_hbm), channel_id=1, source_target_pairs={{0,128},{128,256},{256,384},{384,0},{1,129},{129,257},{257,385},{3... | collective-permute-start | bytes 7077896 | tf_op jit(solution)/shard_map/ppermute | solution.py:18
  50.8 2.1 collective-permute-start.7
  52.9 4.7 %collective-permute-done = bf16[16,2176]{1,0:T(8,128)(2,1)S(1)} collective-permute-done((bf16[16,2176]{1,0:T(8,128)(2,1)S(1)}, bf16[16,2176]{1,0:T(8,128)(2,1)S(1)}, u32[]{:S(2)}, u32[]{:S(2)}) %collective-permute-start) | collective-permute-done | bytes 69664 | tf_op jit(solution)/shard_map/ppermute | solution.py:18
  57.6 2.2 collective-permute-done.1
  59.8 9.5 %collective-permute-done.2 = bf16[16,2176]{1,0:T(8,128)(2,1)S(1)} collective-permute-done((bf16[16,2176]{1,0:T(8,128)(2,1)S(1)}, bf16[16,2176]{1,0:T(8,128)(2,1)S(1)}, u32[]{:S(2)}, u32[]{:S(2)}) %collective-permute-start.2) | collective-permute-done | bytes 69664 | tf_op jit(solution)/shard_map/ppermute | solution.py:18
  69.4 1.9 collective-permute-start.3
  71.3 3.4 %collective-permute-start.4 = (bf16[64,2176]{1,0:T(8,128)(2,1)S(1)}, bf16[64,2176]{1,0:T(8,128)(2,1)}, u32[]{:S(2)}, u32[]{:S(2)}) collective-permute-start(bf16[64,2176]{1,0:T(8,128)(2,1)S(1)} %pad_maximum_fusion.2.refs_1_), channel_id=1, source_target_pairs={{0,120},{8,0},{16,8},{24,16},{32,24},{40,32},{48,40},{56,48},{64,5... | collective-permute-start | bytes 835592 | tf_op jit(solution)/shard_map/ppermute | solution.py:18
  74.7 1.9 collective-permute-start.5
  76.6 1.2 collective-permute-done.3.refs_2_
  77.8 2.2 collective-permute-done.4.refs_3_
  80.0 12.9 %collective-permute-done.5.refs_4_ = bf16[64,2176]{1,0:T(8,128)(2,1)} collective-permute-done((bf16[64,2176]{1,0:T(8,128)(2,1)S(1)}, bf16[64,2176]{1,0:T(8,128)(2,1)}, u32[]{:S(2)}, u32[]{:S(2)}) %collective-permute-start.5) | collective-permute-done | bytes 278560 | tf_op jit(solution)/shard_map/ppermute | solution.py:18
  93.0 3.4 %select_rows.1 = bf16[256,2048]{1,0:T(8,128)(2,1)} custom-call(s32[1]{0:T(128)} %bitcast.30.refs_0_, bf16[64,2176]{1,0:T(8,128)(2,1)} %copy-done.4, bf16[64,2176]{1,0:T(8,128)(2,1)} %collective-permute-done.3.refs_2_, bf16[64,2176]{1,0:T(8,128)(2,1)} %collective-permute-done.4.refs_3_, bf16[64,2176]{1,0:T(8,128)(2,1)} %collective-permute-done.5.refs_4_), custom_call_target="tpu_custom_call" | custom-call | tf_op jit(solution)/shard_map/select_rows/pallas_call | solution.py:78
  96.4 5.4 %all-to-all-start.2 = ((bf16[8,32,2048]{2,1,0:T(8,128)(2,1)}), bf16[8,32,2048]{2,1,0:T(8,128)(2,1)}, u32[]{:S(2)}, u32[]{:S(2)}) async-start(bf16[8,32,2048]{2,1,0:T(8,128)(2,1)} %bitcast.87), calls=%async_computation.2 | async-start | bytes 2097152 | tf_op jit(solution)/shard_map/all_to_all | solution.py:309
  101.8 3.3 %resample.1 = bf16[128,2,1024]{2,1,0:T(2,128)(2,1)} custom-call(bf16[128,2,1152]{2,1,0:T(2,128)(2,1)} %copy-done.2), custom_call_target="tpu_custom_call" | custom-call | tf_op jit(solution)/shard_map/resample/pallas_call | solution.py:171
  105.1 11.8 %all-to-all-done.2 = bf16[8,32,2048]{2,1,0:T(8,128)(2,1)} async-done(((bf16[8,32,2048]{2,1,0:T(8,128)(2,1)}), bf16[8,32,2048]{2,1,0:T(8,128)(2,1)}, u32[]{:S(2)}, u32[]{:S(2)}) %all-to-all-start.2) | async-done | bytes 1048608 | tf_op jit(solution)/shard_map/all_to_all | solution.py:309
  116.9 7.6 %all-to-all-start.1 = ((bf16[128,2,1024]{2,1,0:T(2,128)(2,1)}), bf16[128,2,1024]{2,1,0:T(2,128)(2,1)S(1)}, u32[]{:S(2)}, u32[]{:S(2)}) async-start(bf16[128,2,1024]{2,1,0:T(2,128)(2,1)} %resample.1), calls=%async_computation.1 | async-start | bytes 1048576 | tf_op jit(solution)/shard_map/all_to_all | solution.py:285
  124.5 1.4 slice.34
  125.9 3.2 %collective-permute-start.8 = (bf16[288,2048]{1,0:T(8,128)(2,1)S(1)}, bf16[288,2048]{1,0:T(8,128)(2,1)S(1)}, u32[]{:S(2)}, u32[]{:S(2)}) collective-permute-start(bf16[288,2048]{1,0:T(8,128)(2,1)S(1)} %slice.34), channel_id=1, source_target_pairs={{0,128},{128,256},{256,384},{384,0},{1,129},{129,257},{257,385},{3... | collective-permute-start | bytes 3538952 | tf_op jit(solution)/shard_map/ppermute | solution.py:18
  129.1 1.4 slice.35
  130.5 2.3 collective-permute-start.9
  132.8 22.1 %collective-permute-done.8.low_hbm = bf16[288,2048]{1,0:T(8,128)(2,1)S(1)} collective-permute-done((bf16[288,2048]{1,0:T(8,128)(2,1)S(1)}, bf16[288,2048]{1,0:T(8,128)(2,1)S(1)}, u32[]{:S(2)}, u32[]{:S(2)}) %collective-permute-start.8) | collective-permute-done | bytes 1179680 | tf_op jit(solution)/shard_map/ppermute | solution.py:18
  154.9 4.3 %collective-permute-done.9.high_hbm = bf16[288,2048]{1,0:T(8,128)(2,1)S(1)} collective-permute-done((bf16[288,2048]{1,0:T(8,128)(2,1)S(1)}, bf16[288,2048]{1,0:T(8,128)(2,1)S(1)}, u32[]{:S(2)}, u32[]{:S(2)}) %collective-permute-start.9) | collective-permute-done | bytes 1179680 | tf_op jit(solution)/shard_map/ppermute | solution.py:18
  159.2 6.6 %expert.1 = bf16[128,2,2048]{2,1,0:T(2,128)(2,1)S(1)} custom-call(bf16[256,2048]{1,0:T(8,128)(2,1)} %bitcast.33.rows_hbm, bf16[576,2048]{1,0:T(8,128)(2,1)S(1)} %pad_maximum_fusion.own_hbm, bf16[576,2048]{1,0:T(8,128)(2,1)} %collective-permute-done.6.before_hbm, bf16[576,2048]{1,0:T(8,128)(2,1)} %collective-permute-done.7.after_hbm, ...), custom_call_target="tpu_custom_call" | custom-call | tf_op jit(solution)/shard_map/expert/pallas_call | solution.py:136
  166.9 17.4 %all-to-all-start.3 = ((bf16[128,2,2048]{2,1,0:T(2,128)(2,1)}), bf16[128,2,2048]{2,1,0:T(2,128)(2,1)S(1)}, u32[]{:S(2)}, u32[]{:S(2)}) async-start(bf16[128,2,2048]{2,1,0:T(2,128)(2,1)} %copy-done.1), calls=%async_computation.3 | async-start | bytes 2097152 | tf_op jit(solution)/shard_map/all_to_all | solution.py:321
  194.8 45.1 %all-to-all-done.3 = bf16[128,2,2048]{2,1,0:T(2,128)(2,1)S(1)} async-done(((bf16[128,2,2048]{2,1,0:T(2,128)(2,1)}), bf16[128,2,2048]{2,1,0:T(2,128)(2,1)S(1)}, u32[]{:S(2)}, u32[]{:S(2)}) %all-to-all-start.3) | async-done | bytes 1048608 | tf_op jit(solution)/shard_map/all_to_all | solution.py:321
  (74 shorter events, 15.4 us)
Async XLA Ops:
  0.6 185.5 %copy-start = (bf16[8,2,64,128]{3,2,1,0:T(8,128)(2,1)S(1)}, bf16[8,2,64,128]{3,2,1,0:T(8,128)(2,1)}, u32[]{:S(2)}) copy-start(bf16[8,2,64,128]{3,2,1,0:T(8,128)(2,1)} %param.14) | copy-start | bytes 786436
  2.8 21.3 %copy-start.6 = (bf16[8,2,2048]{2,1,0:T(2,128)(2,1)S(1)}, bf16[8,2,2048]{2,1,0:T(2,128)(2,1)}, u32[]{:S(2)}) copy-start(bf16[8,2,2048]{2,1,0:T(2,128)(2,1)} %param.16) | copy-start | bytes 196612
  2.8 22.3 %copy-start.10 = (f32[2048]{0:T(1024)S(1)}, f32[2048]{0:T(1024)}, u32[]{:S(2)}) copy-start(f32[2048]{0:T(1024)} %param.17) | copy-start | bytes 24580
  4.8 91.5 %all-to-all-start = ((bf16[128,2,1152]{2,1,0:T(2,128)(2,1)}), bf16[128,2,1152]{2,1,0:T(2,128)(2,1)S(1)}, u32[]{:S(2)}, u32[]{:S(2)}) async-start(bf16[128,2,1152]{2,1,0:T(2,128)(2,1)} %pad_maximum_fusion.1), calls=%async_computation | async-start | bytes 1179648 | tf_op jit(solution)/shard_map/all_to_all | solution.py:283
  25.3 32.3 %collective-permute-start = (bf16[16,2176]{1,0:T(8,128)(2,1)S(1)}, bf16[16,2176]{1,0:T(8,128)(2,1)S(1)}, u32[]{:S(2)}, u32[]{:S(2)}) collective-permute-start(bf16[16,2176]{1,0:T(8,128)(2,1)S(1)} %pad_maximum_fusion.3), channel_id=1, source_target_pairs={{0,32},{8,40},{16,48},{24,56},{32,64},{40,72},{48,80},{56,88},{64,... | collective-permute-start | bytes 208904 | tf_op jit(solution)/shard_map/ppermute | solution.py:18
  32.4 27.4 %collective-permute-start.1 = (bf16[16,2176]{1,0:T(8,128)(2,1)S(1)}, bf16[16,2176]{1,0:T(8,128)(2,1)S(1)}, u32[]{:S(2)}, u32[]{:S(2)}) collective-permute-start(bf16[16,2176]{1,0:T(8,128)(2,1)S(1)} %pad_maximum_fusion.3), channel_id=1, source_target_pairs={{0,96},{8,104},{16,112},{24,120},{32,0},{40,8},{48,16},{56,24},{64... | collective-permute-start | bytes 208904 | tf_op jit(solution)/shard_map/ppermute | solution.py:18
  34.5 34.9 %collective-permute-start.2 = (bf16[16,2176]{1,0:T(8,128)(2,1)S(1)}, bf16[16,2176]{1,0:T(8,128)(2,1)S(1)}, u32[]{:S(2)}, u32[]{:S(2)}) collective-permute-start(bf16[16,2176]{1,0:T(8,128)(2,1)S(1)} %pad_maximum_fusion.3), channel_id=1, source_target_pairs={{0,64},{8,72},{16,80},{24,88},{32,96},{40,104},{48,112},{56,120},{... | collective-permute-start | bytes 208904 | tf_op jit(solution)/shard_map/ppermute | solution.py:18
  47.6 76.9 %collective-permute-start.6 = (bf16[576,2048]{1,0:T(8,128)(2,1)S(1)}, bf16[576,2048]{1,0:T(8,128)(2,1)}, u32[]{:S(2)}, u32[]{:S(2)}) collective-permute-start(bf16[576,2048]{1,0:T(8,128)(2,1)S(1)} %pad_maximum_fusion.own_hbm), channel_id=1, source_target_pairs={{0,128},{128,256},{256,384},{384,0},{1,129},{129,257},{257,385},{3... | collective-permute-start | bytes 7077896 | tf_op jit(solution)/shard_map/ppermute | solution.py:18
  50.8 78.3 %collective-permute-start.7 = (bf16[576,2048]{1,0:T(8,128)(2,1)S(1)}, bf16[576,2048]{1,0:T(8,128)(2,1)}, u32[]{:S(2)}, u32[]{:S(2)}) collective-permute-start(bf16[576,2048]{1,0:T(8,128)(2,1)S(1)} %pad_maximum_fusion.own_hbm), channel_id=1, source_target_pairs={{0,384},{128,0},{256,128},{384,256},{1,385},{129,1},{257,129},{385... | collective-permute-start | bytes 7077896 | tf_op jit(solution)/shard_map/ppermute | solution.py:18
  69.3 23.6 %copy-start.4 = (bf16[64,2176]{1,0:T(8,128)(2,1)}, bf16[64,2176]{1,0:T(8,128)(2,1)S(1)}, u32[]{:S(2)}) copy-start(bf16[64,2176]{1,0:T(8,128)(2,1)S(1)} %pad_maximum_fusion.2.refs_1_) | copy-start | bytes 835588
  69.4 8.5 %collective-permute-start.3 = (bf16[64,2176]{1,0:T(8,128)(2,1)S(1)}, bf16[64,2176]{1,0:T(8,128)(2,1)}, u32[]{:S(2)}, u32[]{:S(2)}) collective-permute-start(bf16[64,2176]{1,0:T(8,128)(2,1)S(1)} %pad_maximum_fusion.2.refs_1_), channel_id=1, source_target_pairs={{0,8},{8,16},{16,24},{24,32},{32,40},{40,48},{48,56},{56,64},{64,7... | collective-permute-start | bytes 835592 | tf_op jit(solution)/shard_map/ppermute | solution.py:18
  71.3 8.8 %collective-permute-start.4 = (bf16[64,2176]{1,0:T(8,128)(2,1)S(1)}, bf16[64,2176]{1,0:T(8,128)(2,1)}, u32[]{:S(2)}, u32[]{:S(2)}) collective-permute-start(bf16[64,2176]{1,0:T(8,128)(2,1)S(1)} %pad_maximum_fusion.2.refs_1_), channel_id=1, source_target_pairs={{0,120},{8,0},{16,8},{24,16},{32,24},{40,32},{48,40},{56,48},{64,5... | collective-permute-start | bytes 835592 | tf_op jit(solution)/shard_map/ppermute | solution.py:18
  74.7 18.3 %collective-permute-start.5 = (bf16[64,2176]{1,0:T(8,128)(2,1)S(1)}, bf16[64,2176]{1,0:T(8,128)(2,1)}, u32[]{:S(2)}, u32[]{:S(2)}) collective-permute-start(bf16[64,2176]{1,0:T(8,128)(2,1)S(1)} %pad_maximum_fusion.2.refs_1_), channel_id=1, source_target_pairs={{0,16},{8,24},{16,32},{24,40},{32,48},{40,56},{48,64},{56,72},{64,... | collective-permute-start | bytes 835592 | tf_op jit(solution)/shard_map/ppermute | solution.py:18
  96.4 5.4 %copy-start.2 = (bf16[128,2,1152]{2,1,0:T(2,128)(2,1)}, bf16[128,2,1152]{2,1,0:T(2,128)(2,1)S(1)}, u32[]{:S(2)}) copy-start(bf16[128,2,1152]{2,1,0:T(2,128)(2,1)S(1)} %all-to-all-done.pieces_any) | copy-start | bytes 1769476
  96.4 20.5 %all-to-all-start.2 = ((bf16[8,32,2048]{2,1,0:T(8,128)(2,1)}), bf16[8,32,2048]{2,1,0:T(8,128)(2,1)}, u32[]{:S(2)}, u32[]{:S(2)}) async-start(bf16[8,32,2048]{2,1,0:T(8,128)(2,1)} %bitcast.87), calls=%async_computation.2 | async-start | bytes 2097152 | tf_op jit(solution)/shard_map/all_to_all | solution.py:309
  116.9 50.0 %all-to-all-start.1 = ((bf16[128,2,1024]{2,1,0:T(2,128)(2,1)}), bf16[128,2,1024]{2,1,0:T(2,128)(2,1)S(1)}, u32[]{:S(2)}, u32[]{:S(2)}) async-start(bf16[128,2,1024]{2,1,0:T(2,128)(2,1)} %resample.1), calls=%async_computation.1 | async-start | bytes 1048576 | tf_op jit(solution)/shard_map/all_to_all | solution.py:285
  125.9 29.0 %collective-permute-start.8 = (bf16[288,2048]{1,0:T(8,128)(2,1)S(1)}, bf16[288,2048]{1,0:T(8,128)(2,1)S(1)}, u32[]{:S(2)}, u32[]{:S(2)}) collective-permute-start(bf16[288,2048]{1,0:T(8,128)(2,1)S(1)} %slice.34), channel_id=1, source_target_pairs={{0,128},{128,256},{256,384},{384,0},{1,129},{129,257},{257,385},{3... | collective-permute-start | bytes 3538952 | tf_op jit(solution)/shard_map/ppermute | solution.py:18
  130.5 28.8 %collective-permute-start.9 = (bf16[288,2048]{1,0:T(8,128)(2,1)S(1)}, bf16[288,2048]{1,0:T(8,128)(2,1)S(1)}, u32[]{:S(2)}, u32[]{:S(2)}) collective-permute-start(bf16[288,2048]{1,0:T(8,128)(2,1)S(1)} %slice.35), channel_id=1, source_target_pairs={{0,384},{128,0},{256,128},{384,256},{1,385},{129,1},{257,129},{385... | collective-permute-start | bytes 3538952 | tf_op jit(solution)/shard_map/ppermute | solution.py:18
  159.2 26.3 %copy-start.8 = (bf16[8,2,2,4,128]{4,3,2,1,0:T(4,128)(2,1)S(1)}, bf16[8,2,2,4,128]{4,3,2,1,0:T(4,128)(2,1)}, u32[]{:S(2)}) copy-start(bf16[8,2,2,4,128]{4,3,2,1,0:T(4,128)(2,1)} %param.15) | copy-start | bytes 98308
  165.9 1.0 copy-start.1
  166.9 20.1 %copy-start.5 = (bf16[256,2,4,128]{3,2,1,0:T(4,128)(2,1)S(1)}, bf16[256,2,4,128]{3,2,1,0:T(4,128)(2,1)}, u32[]{:S(2)}) copy-start(bf16[256,2,4,128]{3,2,1,0:T(4,128)(2,1)} %param.12) | copy-start | bytes 1572868
  166.9 73.0 %all-to-all-start.3 = ((bf16[128,2,2048]{2,1,0:T(2,128)(2,1)}), bf16[128,2,2048]{2,1,0:T(2,128)(2,1)S(1)}, u32[]{:S(2)}, u32[]{:S(2)}) async-start(bf16[128,2,2048]{2,1,0:T(2,128)(2,1)} %copy-done.1), calls=%async_computation.3 | async-start | bytes 2097152 | tf_op jit(solution)/shard_map/all_to_all | solution.py:321
  190.5 2.5 %copy-start.3 = (bf16[8,32,2,4,128]{4,3,2,1,0:T(4,128)(2,1)}, bf16[8,32,2,4,128]{4,3,2,1,0:T(4,128)(2,1)S(1)}, u32[]{:S(2)}) copy-start(bf16[8,32,2,4,128]{4,3,2,1,0:T(4,128)(2,1)S(1)} %reshape.117) | copy-start | bytes 1572868
  190.5 1.8 copy-start.7
  193.0 0.7 copy-start.9

commit v5 on v4

--- a/solution.py
+++ b/solution.py
@@ -9,9 +9,8 @@
 from jax.sharding import PartitionSpec as P
 
 
-EP = ("wide", "near", "ep_1", "ep_2")
+EP = ("ep_0", "ep_1", "ep_2")
 REP_EP = ("rep",) + EP
-PLANES = EP[:2]
 
 
 def shift(block, axis, count, step):
@@ -27,66 +26,58 @@
     return before, after, far_low, far_high
 
 
-def ring_rows(block):
-    wide = [block] + [shift(block, PLANES, 16, step) for step in (4, -4, 8)]
-    wide = jnp.concatenate(wide, axis=0)
-    return [wide] + [shift(wide, PLANES, 16, step) for step in (1, -1, 2)]
-
-
-def select_body(place_ref, own_ref, back_ref, ahead_ref, far_ref, out_ref, rows_ref, sems, *, width):
-    copies = [
-        pltpu.make_async_copy(part, rows_ref.at[n * 64 : (n + 1) * 64], sems.at[n])
-        for n, part in enumerate((own_ref, back_ref, ahead_ref, far_ref))
-    ]
-    for copy in copies:
-        copy.start()
-    for copy in copies:
-        copy.wait()
-    count = rows_ref.shape[0]
-    slots = out_ref.shape[0]
-    place = place_ref[0]
-    row = lax.broadcasted_iota(jnp.int32, (count, 1), 0)
-    near, wide = row // 64, row // 16 % 4
-    distance = jnp.where(near == 1, -1, jnp.where(near == 2, 1, jnp.where(near == 3, -2, 0)))
-    distance += jnp.where(wide == 1, -4, jnp.where(wide == 2, 4, jnp.where(wide == 3, -8, 0)))
-    source = (place + distance + 16) % 16
-    column = lax.broadcasted_iota(jnp.int32, (count, slots), 1)
-    expert = place * 8 + column // 32
-    ids = rows_ref[:, width:].astype(jnp.int32)
-    named = ids[:, 0:1] == expert
-    for k in range(1, 8):
-        named = named | (ids[:, k : k + 1] == expert)
-    lower = lax.broadcasted_iota(jnp.int32, (count, count), 0)
-    upper = lax.broadcasted_iota(jnp.int32, (count, count), 1)
-    earlier = (upper < lower) & (upper // 16 == lower // 16)
-    rank = jnp.dot(
-        earlier.astype(jnp.float32).astype(jnp.bfloat16),
-        named.astype(jnp.float32).astype(jnp.bfloat16),
-        preferred_element_type=jnp.float32,
-    ).astype(jnp.int32)
-    chosen = named & (source * 2 + rank == column % 32)
-    out_ref[...] = lax.dot_general(
-        chosen.astype(jnp.float32).astype(jnp.bfloat16),
-        rows_ref[:, :width],
-        (((0,), (0,)), ((), ())),
-        preferred_element_type=jnp.float32,
-    ).astype(jnp.bfloat16)
-
-
-def select_rows(place, blocks, width, slots):
-    rows = sum(b.shape[0] for b in blocks)
+def pack_body(tokens, gain, routes, cache, side, out_ref):
+    width = tokens.shape[2]
+    rows = tokens.shape[0] * tokens.shape[1]
+    devices, two, _ = out_ref.shape
+    slots = devices * two
+    values = tokens[...].astype(jnp.float32).reshape(rows, width)
+    scale = lax.rsqrt(jnp.mean(values * values, axis=-1, keepdims=True) + 1e-06)
+    normed = (values * scale * gain[...]).astype(jnp.bfloat16)
+    slot = lax.broadcasted_iota(jnp.int32, (rows, slots), 1)
+    ids = routes[...]
+    named = ids[:, 0:1] == slot // 2
+    for k in range(1, ids.shape[1]):
+        named = named | (ids[:, k : k + 1] == slot // 2)
+    named = named.astype(jnp.float32)
+    earlier = lax.broadcasted_iota(jnp.int32, (rows, rows), 1) < lax.broadcasted_iota(
+        jnp.int32, (rows, rows), 0
+    )
+    rank = jnp.dot(earlier.astype(jnp.float32), named, preferred_element_type=jnp.float32)
+    chosen = jnp.where(rank.astype(jnp.int32) == slot % 2, named, 0.0).astype(jnp.bfloat16)
+    picked = lax.dot_general(
+        chosen, normed, (((0,), (0,)), ((), ())), preferred_element_type=jnp.float32
+    )
+    out_ref[:, :, :width] = picked.astype(jnp.bfloat16).reshape(devices, two, width)
+    half = cache.shape[0] // 2
+    to = lax.broadcasted_iota(jnp.int32, (slots, devices), 0)
+    come = lax.broadcasted_iota(jnp.int32, (slots, devices), 1)
+    woven = None
+    for k in range(two):
+        wide = jnp.concatenate([cache[k * half + m] for m in range(half)], axis=1)
+        place = (to == come * 2 + k).astype(jnp.float32).astype(jnp.bfloat16)
+        part = jnp.dot(place, wide, preferred_element_type=jnp.float32)
+        woven = part if woven is None else woven + part
+    length = woven.shape[1]
+    out_ref[:, :, width : width + length] = (
+        woven.astype(jnp.bfloat16).reshape(devices, two, length)
+    )
+    out_ref[:, :, width + length :] = jnp.broadcast_to(
+        side[...].reshape(1, two, side.shape[1]), (devices, two, side.shape[1])
+    )
+
+
+def pack(tokens, gain, routes, cache, side):
+    width = tokens.shape[2]
+    total = width + cache.shape[0] * cache.shape[2] // 2 + side.shape[1]
+    spec = pl.BlockSpec(memory_space=pltpu.VMEM)
     return pl.pallas_call(
-        lambda *refs: select_body(*refs, width=width),
-        out_shape=jax.ShapeDtypeStruct((slots, width), jnp.bfloat16),
-        in_specs=[pl.BlockSpec(memory_space=pltpu.SMEM)]
-        + [pl.BlockSpec(memory_space=pl.ANY)] * 4,
-        out_specs=pl.BlockSpec(memory_space=pltpu.VMEM),
-        scratch_shapes=[
-            pltpu.VMEM((rows, blocks[0].shape[1]), jnp.bfloat16),
-            pltpu.SemaphoreType.DMA((4,)),
-        ],
-        name="select_rows",
-    )(place.reshape(1), *blocks)
+        pack_body,
+        out_shape=jax.ShapeDtypeStruct((cache.shape[1], 2, total), jnp.bfloat16),
+        in_specs=[spec] * 5,
+        out_specs=spec,
+        name="pack",
+    )(tokens, gain.reshape(1, width), routes, cache, side)
 
 
 def expert_body(
@@ -99,7 +90,7 @@
         pltpu.make_async_copy(src, dst, sems.at[n])
         for n, (src, dst) in enumerate(
             (
-                (rows_hbm, rows),
+                (rows_hbm.at[:, :, : rows.shape[2]], rows),
                 (own_hbm, own),
                 (before_hbm, before),
                 (after_hbm, after),
@@ -110,35 +101,31 @@
     ]
     for copy in copies:
         copy.start()
-    count = rows.shape[0]
-    to = lax.broadcasted_iota(jnp.int32, (count, count), 0)
-    come = lax.broadcasted_iota(jnp.int32, (count, count), 1)
-    order = come == to // 2 % 8 * 32 + to // 16 * 2 + to % 2
-    order = order.astype(jnp.float32).astype(jnp.bfloat16)
     total = None
     contract = (((1,), (1,)), ((), ()))
     for weights, waits in ((own, (0, 1)), (before, (2,)), (after, (3,)), (far, (4, 5))):
         for n in waits:
             copies[n].wait()
+        if total is None:
+            tokens = rows[...].reshape(rows.shape[0] * rows.shape[1], rows.shape[2])
         both = lax.dot_general(
-            rows[...], weights[: 2 * hidden], contract, preferred_element_type=jnp.float32
+            tokens, weights[: 2 * hidden], contract, preferred_element_type=jnp.float32
         )
         gate, upward = both[:, :hidden], both[:, hidden:]
         act = (gate / (1.0 + jnp.exp(-gate)) * upward).astype(jnp.bfloat16)
-        act = jnp.dot(order, act, preferred_element_type=jnp.float32).astype(jnp.bfloat16)
         part = jnp.dot(act, weights[2 * hidden :], preferred_element_type=jnp.float32)
         total = part if total is None else total + part
     result[...] = total.astype(jnp.bfloat16).reshape(result.shape)
 
 
 def expert(rows, own, before, after, low, high):
-    count, width = rows.shape
+    count, width = 2 * rows.shape[0], own.shape[1]
     return pl.pallas_call(
         expert_body,
         out_shape=jax.ShapeDtypeStruct((count // 2, 2, width), jnp.bfloat16),
         in_specs=[pl.BlockSpec(memory_space=pl.ANY)] + [pl.BlockSpec(memory_space=pltpu.HBM)] * 5,
         out_specs=pl.BlockSpec(memory_space=pltpu.VMEM),
-        scratch_shapes=[pltpu.VMEM((count, width), jnp.bfloat16)]
+        scratch_shapes=[pltpu.VMEM((count // 2, 2, width), jnp.bfloat16)]
         + [pltpu.VMEM(own.shape, jnp.bfloat16)] * 4
         + [pltpu.SemaphoreType.DMA((6,))],
         compiler_params=pltpu.CompilerParams(vmem_limit_bytes=32 * 1024 * 1024),
@@ -147,7 +134,8 @@
 
 
 def resample_body(pieces_any, out_ref, pieces_ref, sem):
-    copy = pltpu.make_async_copy(pieces_any, pieces_ref, sem)
+    first = pieces_any.shape[2] - pieces_ref.shape[2]
+    copy = pltpu.make_async_copy(pieces_any.at[:, :, first:], pieces_ref, sem)
     copy.start()
     copy.wait()
     devices, two, width = pieces_ref.shape
@@ -173,7 +161,10 @@
         out_shape=jax.ShapeDtypeStruct(pieces.shape[:2] + (length,), jnp.bfloat16),
         in_specs=[pl.BlockSpec(memory_space=pl.ANY)],
         out_specs=pl.BlockSpec(memory_space=pltpu.VMEM),
-        scratch_shapes=[pltpu.VMEM(pieces.shape, jnp.bfloat16), pltpu.SemaphoreType.DMA(())],
+        scratch_shapes=[
+            pltpu.VMEM(pieces.shape[:2] + (length + 128,), jnp.bfloat16),
+            pltpu.SemaphoreType.DMA(()),
+        ],
         name="resample",
     )(pieces)
 
@@ -255,7 +246,6 @@
 ):
     ep_count = lax.axis_size(EP)
     per_dev = gen_cache.shape[0]
-    row_count = 2 * per_dev
     width = tokens_in.shape[2]
     top_count = routes.shape[3]
     half_cols = w_down.shape[1]
@@ -267,53 +257,30 @@
     own = jnp.concatenate([in_own, out_own], axis=0)
     before, after, low, high = ring_gather(own)
 
+    rep_place = lax.axis_index("rep")
+    own_routes = lax.dynamic_index_in_dim(routes, rep_place, 0, keepdims=False).reshape(
+        -1, top_count
+    )
+    own_gates = lax.dynamic_index_in_dim(gate_weights, rep_place, 0, keepdims=False).reshape(
+        -1, top_count
+    )
     piece_len = gen_cache.size // (per_dev * ep_count)
-    flat_cache = (
-        gen_cache.reshape(per_dev, ep_count, piece_len)
-        .transpose(1, 0, 2)
-        .reshape(ep_count, 2, per_dev * piece_len // 2)
-    )
-    flat_len = flat_cache.shape[2]
+    flat_len = per_dev * piece_len // 2
     fours = ancestors.reshape(2, per_dev // 2)
     digits = jnp.concatenate([fours // 256, fours % 256], axis=1).astype(jnp.bfloat16)
     side = jnp.pad(digits, ((0, 0), (0, 128 - digits.shape[1])))
-    flat_cache = jnp.concatenate(
-        [flat_cache, jnp.broadcast_to(side, (ep_count,) + side.shape)], axis=2
-    )
-    pieces = lax.all_to_all(flat_cache, EP, split_axis=0, concat_axis=0, tiled=True)
-    chosen = resample(pieces, flat_len)
+    outgoing = pack(
+        tokens_in, norm_gain, own_routes, gen_cache.reshape(per_dev, ep_count, piece_len), side
+    )
+    received = lax.all_to_all(outgoing, EP, split_axis=0, concat_axis=0, tiled=True)
+    chosen = resample(received, flat_len)
     moved = lax.all_to_all(chosen, EP, split_axis=0, concat_axis=0, tiled=True)
     cache_out = (
         moved.reshape(ep_count, per_dev, piece_len).transpose(1, 0, 2).reshape(gen_cache.shape)
     )
     attn_out = attend(queries, cache_out, new_kv, prompt_cache)
 
-    values_f = tokens_in.astype(jnp.float32).reshape(row_count, width)
-    normed = (
-        values_f
-        * lax.rsqrt(jnp.mean(values_f * values_f, axis=-1, keepdims=True) + 1e-06)
-        * norm_gain
-    ).astype(jnp.bfloat16)
-    rep_place = lax.axis_index("rep")
-    own_routes = lax.dynamic_index_in_dim(routes, rep_place, 0, keepdims=False).reshape(
-        -1, top_count
-    )
-    own_gates = lax.dynamic_index_in_dim(gate_weights, rep_place, 0, keepdims=False).reshape(
-        -1, top_count
-    )
-    labels = jnp.pad(own_routes.astype(jnp.bfloat16), ((0, 0), (0, 128 - top_count)))
-    blocks = ring_rows(jnp.concatenate([normed, labels], axis=1))
-    planes = lax.axis_size(PLANES)
-    local = ep_count // planes
-    packed = select_rows(lax.axis_index(PLANES), blocks, width, slot_count)
-    rows = lax.all_to_all(
-        packed.reshape(local, planes * per_expert, width),
-        EP[2:],
-        split_axis=0,
-        concat_axis=0,
-        tiled=True,
-    ).reshape(slot_count, width)
-    produced = expert(rows, own, before, after, low, high)
+    produced = expert(received, own, before, after, low, high)
 
     slot_ids = slot_numbers(own_routes, per_expert)
     hits = jnp.arange(slot_count, dtype=jnp.int32)[:, None, None] == slot_ids[None, :, :]
@@ -331,7 +298,7 @@
 
 
 def solution(mesh):
-    torus = Mesh(mesh.devices.reshape(mesh.shape["rep"], 4, 4, 4, 2), REP_EP)
+    torus = Mesh(mesh.devices.reshape(mesh.shape["rep"], 16, 4, 2), REP_EP)
     placed = (
         P(REP_EP, None, None, None, None),
         P(),

time: 243 us -> 238 us (0.979)
  starting transfers between devices: 88.1 us -> 54.5 us
  waiting for transfers between devices: 116 us -> 144 us
    all_to_all x2 -> x1, waiting for transfers between devices: 11.8 us -> 72.2 us  [shards(): lax.all_to_all(outgoing, EP, split_axis=0, concat_axis=0, tiled=True)]
    ppermute x10 -> x4, waiting for transfers between devices: 59.3 us -> 26.7 us  [shift(): lax.ppermute(block, axis, [(i, (i + step) % count) for i in range(count)])]
    ppermute x10 -> x4, starting transfers between devices: 38.4 us -> 10.7 us  [shift(): lax.ppermute(block, axis, [(i, (i + step) % count) for i in range(count)])]
    all_to_all x2 -> x1, starting transfers between devices: 24.7 us -> 19.3 us  [shards(): lax.all_to_all(outgoing, EP, split_axis=0, concat_axis=0, tiled=True)]
  transfers between devices with their start and end apart: 14 -> 7, of which waited for: 10 -> 4; matrix products, arithmetic and copies ran while one was open for 7% -> 7% of each run, Pallas kernels for 6% -> 4%
where the time goes in v5:
time: 238 us; the launch traced here: 237 us
  waiting for transfers between devices  144 us (61%)
  starting transfers between devices  54.5 us (23%)
  local copies, waits for them, and re-layouts  15.2 us (6%)
  Pallas kernels  14.1 us (6%)
  other arithmetic  4.76 us (2%)
  matrix products  3.72 us (2%)
    all_to_all x1, waiting for transfers between devices, shards(): lax.all_to_all(outgoing, EP, split_axis=0, concat_axis=0, tiled=True)  72.2 us
    all_to_all x1, waiting for transfers between devices, shards(): lax.all_to_all(produced, EP, split_axis=0, concat_axis=0, tiled=True)  45.1 us
    ppermute x4, waiting for transfers between devices, shift(): lax.ppermute(block, axis, [(i, (i + step) % count) for i in range(count)])  26.7 us
    all_to_all x1, starting transfers between devices, shards(): lax.all_to_all(outgoing, EP, split_axis=0, concat_axis=0, tiled=True)  19.3 us
    all_to_all x1, starting transfers between devices, shards(): lax.all_to_all(produced, EP, split_axis=0, concat_axis=0, tiled=True)  17.4 us
    ppermute x4, starting transfers between devices, shift(): lax.ppermute(block, axis, [(i, (i + step) % count) for i in range(count)])  10.7 us
    pallas_call x1, Pallas kernels, expert(): pl.pallas_call(expert_body, out_shape=jax.ShapeDtypeStruct((count // 2, 2...  7.34 us
    all_to_all x1, starting transfers between devices, shards(): moved = lax.all_to_all(chosen, EP, split_axis=0, concat_axis=0, tiled=True)  7.11 us
  transfers between devices with their start and end apart: 7, of which 4 were waited for; matrix products, arithmetic and copies ran while one was open for 7% of the time, Pallas kernels for 4%

profile of v5, /device:TPU:41, one launch (start us, length us, event | category | flops | bytes accessed | tf_op | source)
XLA Modules:
  0.0 237.2 jit_solution(16751456158605382827)
XLA Ops:
  0.6 0.8 reshape.85
  1.4 2.2 reshape.84.cache
  3.6 1.3 constant_dynamic-slice_fusion.1
  4.9 0.6 fusion.20.side
  5.5 3.4 %pack.1 = bf16[128,2,3200]{2,1,0:T(2,128)(2,1)} custom-call(bf16[8,2,2048]{2,1,0:T(2,128)(2,1)} %tokens.1, f32[1,2048]{1,0:T(1,128)} %bitcast.88, s32[16,8]{1,0:T(8,128)} %bitcast.85, bf16[8,128,256]{2,1,0:T(8,128)(2,1)} %reshape.84.cache, bf16[2,128]{1,0:T(2,128)(2,1)} %fusion.20.side), custom_call_target="tpu_custom_call" | custom-call | tf_op jit(solution)/shard_map/pack/pallas_call | solution.py:74
  8.9 19.3 %all-to-all-start = ((bf16[128,2,3200]{2,1,0:T(2,128)(2,1)}), bf16[128,2,3200]{2,1,0:T(2,128)(2,1)S(1)}, u32[]{:S(2)}, u32[]{:S(2)}) async-start(bf16[128,2,3200]{2,1,0:T(2,128)(2,1)} %pack.1), calls=%async_computation | async-start | bytes 3276800 | tf_op jit(solution)/shard_map/all_to_all | solution.py:275
  28.2 2.8 %pad_maximum_fusion.own_hbm = bf16[576,2048]{1,0:T(8,128)(2,1)} fusion(bf16[192,2048]{1,0:T(8,128)(2,1)} %bitcast.83, bf16[384,2048]{1,0:T(8,128)(2,1)S(1)} %bitcast.82), kind=kLoop, calls=%fused_computation | loop fusion | flops 4718592 | bytes 4718592 | tf_op jit(solution)/shard_map/concatenate | solution.py:257
  31.0 3.2 %collective-permute-start = (bf16[576,2048]{1,0:T(8,128)(2,1)}, bf16[576,2048]{1,0:T(8,128)(2,1)}, u32[]{:S(2)}, u32[]{:S(2)}) collective-permute-start(bf16[576,2048]{1,0:T(8,128)(2,1)} %pad_maximum_fusion.own_hbm), channel_id=1, source_target_pairs={{0,128},{128,256},{256,384},{384,0},{1,129},{129,257},{257,385},{3... | collective-permute-start | bytes 7077896 | tf_op jit(solution)/shard_map/ppermute | solution.py:17
  34.2 2.1 collective-permute-start.1
  36.2 72.2 %all-to-all-done.pieces_any.rows_hbm = bf16[128,2,3200]{2,1,0:T(2,128)(2,1)S(1)} async-done(((bf16[128,2,3200]{2,1,0:T(2,128)(2,1)}), bf16[128,2,3200]{2,1,0:T(2,128)(2,1)S(1)}, u32[]{:S(2)}, u32[]{:S(2)}) %all-to-all-start) | async-done | bytes 1638432 | tf_op jit(solution)/shard_map/all_to_all | solution.py:275
  108.5 1.2 copy-done.1
  109.7 3.3 %resample.1 = bf16[128,2,1024]{2,1,0:T(2,128)(2,1)} custom-call(bf16[128,2,3200]{2,1,0:T(2,128)(2,1)} %copy-done.1), custom_call_target="tpu_custom_call" | custom-call | tf_op jit(solution)/shard_map/resample/pallas_call | solution.py:159
  113.0 7.1 %all-to-all-start.1 = ((bf16[128,2,1024]{2,1,0:T(2,128)(2,1)}), bf16[128,2,1024]{2,1,0:T(2,128)(2,1)S(1)}, u32[]{:S(2)}, u32[]{:S(2)}) async-start(bf16[128,2,1024]{2,1,0:T(2,128)(2,1)} %resample.1), calls=%async_computation.1 | async-start | bytes 1048576 | tf_op jit(solution)/shard_map/all_to_all | solution.py:277
  120.2 1.5 slice.34
  121.7 3.2 %collective-permute-start.2 = (bf16[288,2048]{1,0:T(8,128)(2,1)S(1)}, bf16[288,2048]{1,0:T(8,128)(2,1)S(1)}, u32[]{:S(2)}, u32[]{:S(2)}) collective-permute-start(bf16[288,2048]{1,0:T(8,128)(2,1)S(1)} %slice.34), channel_id=1, source_target_pairs={{0,128},{128,256},{256,384},{384,0},{1,129},{129,257},{257,385},{3... | collective-permute-start | bytes 3538952 | tf_op jit(solution)/shard_map/ppermute | solution.py:17
  124.9 1.4 slice.35
  126.3 2.2 collective-permute-start.3
  128.5 22.2 %collective-permute-done.2.low_hbm = bf16[288,2048]{1,0:T(8,128)(2,1)S(1)} collective-permute-done((bf16[288,2048]{1,0:T(8,128)(2,1)S(1)}, bf16[288,2048]{1,0:T(8,128)(2,1)S(1)}, u32[]{:S(2)}, u32[]{:S(2)}) %collective-permute-start.2) | collective-permute-done | bytes 1179680 | tf_op jit(solution)/shard_map/ppermute | solution.py:17
  150.7 4.5 %collective-permute-done.3.high_hbm = bf16[288,2048]{1,0:T(8,128)(2,1)S(1)} collective-permute-done((bf16[288,2048]{1,0:T(8,128)(2,1)S(1)}, bf16[288,2048]{1,0:T(8,128)(2,1)S(1)}, u32[]{:S(2)}, u32[]{:S(2)}) %collective-permute-start.3) | collective-permute-done | bytes 1179680 | tf_op jit(solution)/shard_map/ppermute | solution.py:17
  155.2 7.3 %expert.1 = bf16[128,2,2048]{2,1,0:T(2,128)(2,1)} custom-call(bf16[128,2,3200]{2,1,0:T(2,128)(2,1)S(1)} %copy-done.2, bf16[576,2048]{1,0:T(8,128)(2,1)} %pad_maximum_fusion.own_hbm, bf16[576,2048]{1,0:T(8,128)(2,1)} %collective-permute-done.before_hbm, bf16[576,2048]{1,0:T(8,128)(2,1)} %collective-permute-done.1.after_hbm, ...), custom_call_target="tpu_custom_call" | custom-call | tf_op jit(solution)/shard_map/expert/pallas_call | solution.py:123
  162.6 17.4 %all-to-all-start.2 = ((bf16[128,2,2048]{2,1,0:T(2,128)(2,1)}), bf16[128,2,2048]{2,1,0:T(2,128)(2,1)S(1)}, u32[]{:S(2)}, u32[]{:S(2)}) async-start(bf16[128,2,2048]{2,1,0:T(2,128)(2,1)} %expert.1), calls=%async_computation.2 | async-start | bytes 2097152 | tf_op jit(solution)/shard_map/all_to_all | solution.py:288
  180.4 0.7 constant_dynamic-slice_fusion
  181.2 0.6 fusion.23
  181.8 0.8 fusion.24
  182.6 0.9 fusion.22
  184.1 0.9 copy.184
  185.0 1.2 reshape.87
  188.0 0.7 convolution_bitcast_fusion.2
  188.7 0.7 fusion.2
  189.7 0.7 copy.126
  190.5 45.1 %all-to-all-done.2 = bf16[128,2,2048]{2,1,0:T(2,128)(2,1)S(1)} async-done(((bf16[128,2,2048]{2,1,0:T(2,128)(2,1)}), bf16[128,2,2048]{2,1,0:T(2,128)(2,1)S(1)}, u32[]{:S(2)}, u32[]{:S(2)}) %all-to-all-start.2) | async-done | bytes 1048608 | tf_op jit(solution)/shard_map/all_to_all | solution.py:288
  236.5 0.7 reshape.92
  (45 shorter events, 4.2 us)
Async XLA Ops:
  0.6 181.2 %copy-start = (bf16[8,2,64,128]{3,2,1,0:T(8,128)(2,1)S(1)}, bf16[8,2,64,128]{3,2,1,0:T(8,128)(2,1)}, u32[]{:S(2)}) copy-start(bf16[8,2,64,128]{3,2,1,0:T(8,128)(2,1)} %param.14) | copy-start | bytes 786436
  5.5 22.7 %copy-start.4 = (bf16[1,2048,2,192]{1,3,2,0:T(8,128)(2,1)S(1)}, bf16[1,2048,2,192]{1,3,2,0:T(8,128)(2,1)}, u32[]{:S(2)}) copy-start(bf16[1,2048,2,192]{1,3,2,0:T(8,128)(2,1)} %param.20) | copy-start | bytes 4718596
  8.9 99.6 %all-to-all-start = ((bf16[128,2,3200]{2,1,0:T(2,128)(2,1)}), bf16[128,2,3200]{2,1,0:T(2,128)(2,1)S(1)}, u32[]{:S(2)}, u32[]{:S(2)}) async-start(bf16[128,2,3200]{2,1,0:T(2,128)(2,1)} %pack.1), calls=%async_computation | async-start | bytes 3276800 | tf_op jit(solution)/shard_map/all_to_all | solution.py:275
  31.0 89.2 %collective-permute-start = (bf16[576,2048]{1,0:T(8,128)(2,1)}, bf16[576,2048]{1,0:T(8,128)(2,1)}, u32[]{:S(2)}, u32[]{:S(2)}) collective-permute-start(bf16[576,2048]{1,0:T(8,128)(2,1)} %pad_maximum_fusion.own_hbm), channel_id=1, source_target_pairs={{0,128},{128,256},{256,384},{384,0},{1,129},{129,257},{257,385},{3... | collective-permute-start | bytes 7077896 | tf_op jit(solution)/shard_map/ppermute | solution.py:17
  34.2 90.7 %collective-permute-start.1 = (bf16[576,2048]{1,0:T(8,128)(2,1)}, bf16[576,2048]{1,0:T(8,128)(2,1)}, u32[]{:S(2)}, u32[]{:S(2)}) collective-permute-start(bf16[576,2048]{1,0:T(8,128)(2,1)} %pad_maximum_fusion.own_hbm), channel_id=1, source_target_pairs={{0,384},{128,0},{256,128},{384,256},{1,385},{129,1},{257,129},{385... | collective-permute-start | bytes 7077896 | tf_op jit(solution)/shard_map/ppermute | solution.py:17
  108.5 1.2 copy-start.1
  113.0 49.5 %all-to-all-start.1 = ((bf16[128,2,1024]{2,1,0:T(2,128)(2,1)}), bf16[128,2,1024]{2,1,0:T(2,128)(2,1)S(1)}, u32[]{:S(2)}, u32[]{:S(2)}) async-start(bf16[128,2,1024]{2,1,0:T(2,128)(2,1)} %resample.1), calls=%async_computation.1 | async-start | bytes 1048576 | tf_op jit(solution)/shard_map/all_to_all | solution.py:277
  120.1 35.1 %copy-start.2 = (bf16[128,2,3200]{2,1,0:T(2,128)(2,1)S(1)}, bf16[128,2,3200]{2,1,0:T(2,128)(2,1)}, u32[]{:S(2)}) copy-start(bf16[128,2,3200]{2,1,0:T(2,128)(2,1)} %copy-done.1) | copy-start | bytes 4915204
  121.7 29.0 %collective-permute-start.2 = (bf16[288,2048]{1,0:T(8,128)(2,1)S(1)}, bf16[288,2048]{1,0:T(8,128)(2,1)S(1)}, u32[]{:S(2)}, u32[]{:S(2)}) collective-permute-start(bf16[288,2048]{1,0:T(8,128)(2,1)S(1)} %slice.34), channel_id=1, source_target_pairs={{0,128},{128,256},{256,384},{384,0},{1,129},{129,257},{257,385},{3... | collective-permute-start | bytes 3538952 | tf_op jit(solution)/shard_map/ppermute | solution.py:17
  126.3 53.7 %copy-start.7 = (s32[1,8,2,8]{3,2,1,0:T(2,128)S(1)}, s32[1,8,2,8]{3,2,1,0:T(2,128)}, u32[]{:S(2)}) copy-start(s32[1,8,2,8]{3,2,1,0:T(2,128)} %constant_dynamic-slice_fusion.1) | copy-start | bytes 1540
  126.3 54.9 %copy-start.8 = (bf16[8,2,2,4,128]{4,3,2,1,0:T(4,128)(2,1)S(1)}, bf16[8,2,2,4,128]{4,3,2,1,0:T(4,128)(2,1)}, u32[]{:S(2)}) copy-start(bf16[8,2,2,4,128]{4,3,2,1,0:T(4,128)(2,1)} %param.15) | copy-start | bytes 98308
  126.3 28.9 %collective-permute-start.3 = (bf16[288,2048]{1,0:T(8,128)(2,1)S(1)}, bf16[288,2048]{1,0:T(8,128)(2,1)S(1)}, u32[]{:S(2)}, u32[]{:S(2)}) collective-permute-start(bf16[288,2048]{1,0:T(8,128)(2,1)S(1)} %slice.35), channel_id=1, source_target_pairs={{0,384},{128,0},{256,128},{384,256},{1,385},{129,1},{257,129},{385... | collective-permute-start | bytes 3538952 | tf_op jit(solution)/shard_map/ppermute | solution.py:17
  162.5 20.0 %copy-start.5 = (bf16[256,2,4,128]{3,2,1,0:T(4,128)(2,1)S(1)}, bf16[256,2,4,128]{3,2,1,0:T(4,128)(2,1)}, u32[]{:S(2)}) copy-start(bf16[256,2,4,128]{3,2,1,0:T(4,128)(2,1)} %param.12) | copy-start | bytes 1572868
  162.6 73.0 %all-to-all-start.2 = ((bf16[128,2,2048]{2,1,0:T(2,128)(2,1)}), bf16[128,2,2048]{2,1,0:T(2,128)(2,1)S(1)}, u32[]{:S(2)}, u32[]{:S(2)}) async-start(bf16[128,2,2048]{2,1,0:T(2,128)(2,1)} %expert.1), calls=%async_computation.2 | async-start | bytes 2097152 | tf_op jit(solution)/shard_map/all_to_all | solution.py:288
  186.2 2.5 %copy-start.3 = (bf16[8,32,2,4,128]{4,3,2,1,0:T(4,128)(2,1)}, bf16[8,32,2,4,128]{4,3,2,1,0:T(4,128)(2,1)S(1)}, u32[]{:S(2)}) copy-start(bf16[8,32,2,4,128]{4,3,2,1,0:T(4,128)(2,1)S(1)} %reshape.87) | copy-start | bytes 1572868
  186.2 1.8 copy-start.6
  188.7 0.7 copy-start.9
